TPU v7x, 512 devices: a whole 4x4x16 slice. The times are simulated.
512 devices in a mesh: group: 64 (over y, z_hi, x, core), tensor: 8 (over z_lo).
Axes of the slice: x: 4, y: 4, z: 16 (z_hi: 2, z_lo: 8; z = z_hi * 8 + z_lo), core: 2. Of those that a mesh axis runs over, the one named last changes fastest.
Arguments:
- prompt_cache: bfloat16 [2, 262144, 1024], P(None, ('group', 'tensor')), may hold values from -6 to 6
- queries: bfloat16 [128, 64, 8192], P('group', None, 'tensor'), may hold values from -10 to 10
- new_cache: bfloat16 [2, 128, 64, 1024], P(None, 'group', None, 'tensor'), may hold values from -6 to 6
- offsets: int32 [64, 2], P('group'), may hold values from 0 to 3
- lengths: int32 [64], P('group'), may hold values from 64 to 4096
- block_table: int32 [64, 32], P('group'), may hold values from 0 to 31, each once within a row
Outputs:
- attention: bfloat16 [128, 64, 8192], P('group', None, 'tensor')
Inputs may be any that keep to these rules, and one draw needn't show every extreme that they name: Each row of block_table names each of the 32 stored blocks of its prompt once.
All inputs are finite; a program needn't handle non-finite values.
Results may differ from a plain program's by a relative error of at most 0.0095.
Values may be sent and summed in bfloat16 or wider, within the bound.
No kernel may reach another device: no remote copies, remote signals or barrier semaphores. Data moves between devices by JAX's collectives and lax.ppermute only.
A program may use at most 64 MiB of HBM per device.

v0:
```python
from functools import partial

import jax
import jax.numpy as jnp
from jax import lax
from jax.experimental import pallas as pl
from jax.experimental.pallas import tpu as pltpu
from jax.sharding import PartitionSpec as P


HD = 128
BLOCK = 128
STEPS = 4
REACH = 4
ROW = 8
TAG = 16
PART = 4
HEADS = 8
QROWS = 64
MSG = HEADS * HD + 128
MASKED = -1e30
ORDER = ((0, 4, 1, 5), (2, 6, 3), (7,))
SCALE2 = 1.4426950408889634 * HD ** (-0.5)


def head_rows(q):
    return jnp.concatenate([q[:, h * HD:(h + 1) * HD] for h in range(HEADS)], axis=0)


def scores_of(q, k):
    return lax.dot_general(q, k, (((1,), (1,)), ((), ())), preferred_element_type=jnp.float32) * SCALE2


def split3(x):
    hi = x.astype(jnp.bfloat16).astype(jnp.float32)
    rest = x - hi
    mid = rest.astype(jnp.bfloat16).astype(jnp.float32)
    return hi, mid, rest - mid


def flash_kernel(n_chunks, lo, first, outs_of, wanted_ref, bias_ref, q_ref, *refs):
    k_wide, v_wide = refs[-2:]
    kv_refs = refs[:n_chunks]
    refs = refs[n_chunks:-2]
    if first:
        outs = refs
    else:
        acc_in, top_in = refs[:2]
        outs = refs[2:]
    tokens = kv_refs[0].shape[1]
    step = pl.program_id(0)

    @pl.when(step == 0)
    def _():
        for m in range(n_chunks):
            rows = slice(m * tokens, (m + 1) * tokens)
            k_wide[rows, :HD] = kv_refs[m][0]
            v_wide[rows, :HD] = kv_refs[m][1]
        k_wide[:, HD:] = bias_ref[...]
        v_wide[:, HD:] = jnp.ones((n_chunks * tokens, HD), jnp.bfloat16)

    @pl.when(wanted_ref[lo + step] == 1)
    def _():
        lane = lax.broadcasted_iota(jnp.int32, (1, HD), 1)
        count = PART * QROWS
        mark = jnp.broadcast_to(jnp.where(lane == 0, 1.0, 0.0).astype(jnp.bfloat16), (count, HD))
        parts = []
        stats = jnp.zeros((QROWS, HD), jnp.float32)
        for block in range(HEADS // PART):
            rows = slice(block * count, (block + 1) * count)
            heads = range(block * PART, (block + 1) * PART)
            q = jnp.concatenate([q_ref[0, :, h * HD:(h + 1) * HD] for h in heads], axis=0)
            s = lax.dot_general(
                jnp.concatenate([q, mark], axis=1),
                k_wide[...],
                (((1,), (1,)), ((), ())),
                preferred_element_type=jnp.float32,
            )
            top = jnp.broadcast_to(jnp.max(s, axis=1, keepdims=True), (count, HD))
            if not first:
                old = top_in[0, rows]
                top = jnp.maximum(old, top)
            p = jnp.exp2((s - top[:, 0:1]) * SCALE2).astype(jnp.bfloat16)
            acc = jnp.dot(p, v_wide[...], preferred_element_type=jnp.float32)
            if not first:
                alpha = jnp.exp2((old - top) * SCALE2)
                acc = acc + acc_in[0, rows] * jnp.concatenate([alpha, alpha], axis=1)
            if outs_of is None:
                outs[0][0, rows] = acc
                outs[1][0, rows] = top
                continue
            parts.append((acc[:, :HD] / acc[:, HD:]).astype(jnp.bfloat16))
            big = split3(top * SCALE2 + jnp.log2(acc[:, HD:]))
            for index, h in enumerate(heads):
                mine = slice(index * QROWS, (index + 1) * QROWS)
                for c in range(3):
                    stats = jnp.where(lane == 3 * h + c, big[c][mine], stats)
        if outs_of is None:
            return
        for index, msg in enumerate(outs):
            for slot in range(outs_of):

                @pl.when(step == index * outs_of + slot)
                def _():
                    there = slice(slot * QROWS, (slot + 1) * QROWS)
                    for h in range(HEADS):
                        mine = slice(h % PART * QROWS, (h % PART + 1) * QROWS)
                        msg[there, h * HD:(h + 1) * HD] = parts[h // PART][mine]
                    msg[there, HEADS * HD:] = stats.astype(jnp.bfloat16)


def flash_call(wanted, bias, q_all, chunks, state, slots, caps, last=False):
    first = state is None
    lo, count = slots
    rows = HEADS * QROWS
    n = len(chunks)
    tokens = n * chunks[0].shape[1]
    at = lambda s, w: (lo + s, 0, 0)
    in_specs = [
        pl.BlockSpec(bias.shape, lambda s, w: (0, 0)),
        pl.BlockSpec((1, QROWS, HEADS * HD), lambda s, w: ((lo + s) // caps, (lo + s) % caps, 0)),
    ]
    in_specs += [pl.BlockSpec(c.shape, lambda s, w: (0, 0, 0)) for c in chunks]
    operands = [bias, q_all, *chunks]
    state_specs = [pl.BlockSpec((1, rows, 2 * HD), at), pl.BlockSpec((1, rows, HD), at)]
    if not first:
        in_specs += state_specs
        operands += list(state)
    if not last:
        out_specs = state_specs
        shapes = [(count, rows, 2 * HD), (count, rows, HD)]
        out_shape = [jax.ShapeDtypeStruct(s, jnp.float32) for s in shapes]
    else:
        out_specs = [pl.BlockSpec((caps * QROWS, MSG), lambda s, w: (0, 0))] * (count // caps)
        out_shape = [jax.ShapeDtypeStruct((caps * QROWS, MSG), jnp.bfloat16)] * (count // caps)
    return pl.pallas_call(
        partial(flash_kernel, n, lo, first, caps if last else None),
        grid_spec=pltpu.PrefetchScalarGridSpec(
            num_scalar_prefetch=1,
            grid=(count,),
            in_specs=in_specs,
            out_specs=out_specs,
            scratch_shapes=[pltpu.VMEM((tokens, 2 * HD), jnp.bfloat16)] * 2,
        ),
        out_shape=out_shape,
        compiler_params=pltpu.CompilerParams(dimension_semantics=("arbitrary",)),
        cost_estimate=pl.CostEstimate(
            flops=8 * count * rows * tokens * HD,
            transcendentals=count * rows * tokens,
            bytes_accessed=4 * tokens * HD,
        ),
        name="flash_last" if last else "flash_part",
    )(wanted, *operands)


def own_kernel(q_ref, new_ref, part_ref, stat_ref):
    lane = lax.broadcasted_iota(jnp.int32, (1, HD), 1)
    shape = (HEADS * QROWS, QROWS)
    query = lax.broadcasted_iota(jnp.int32, shape, 0) % QROWS
    token = lax.broadcasted_iota(jnp.int32, shape, 1)
    seen = (query // STEPS == token // STEPS) & (token <= query)
    for slot in range(q_ref.shape[0]):
        q = head_rows(q_ref[slot])
        s = jnp.where(seen, scores_of(q, new_ref[0, slot]), MASKED)
        m = jnp.max(s, axis=1, keepdims=True)
        p = jnp.exp2(s - m)
        l = jnp.sum(p, axis=1, keepdims=True)
        acc = jnp.dot(p.astype(jnp.bfloat16), new_ref[1, slot], preferred_element_type=jnp.float32)
        part = acc / l
        big = m + jnp.log2(l)
        stats = jnp.zeros((QROWS, HD), jnp.float32)
        for h in range(HEADS):
            rows = slice(h * QROWS, (h + 1) * QROWS)
            part_ref[slot, :, h * HD:(h + 1) * HD] = part[rows]
            stats = jnp.where(lane == h, big[rows], stats)
        stat_ref[slot] = stats


def own_call(queries, new_cache):
    slots = queries.shape[0]
    return pl.pallas_call(
        own_kernel,
        out_shape=[
            jax.ShapeDtypeStruct(queries.shape, jnp.float32),
            jax.ShapeDtypeStruct((slots, QROWS, HD), jnp.float32),
        ],
        name="own_part",
    )(queries, new_cache)


def merge_kernel(code_ref, m0, m1, m2, m3, m4, part_ref, stat_ref, out_ref, msg, sem):
    slots = out_ref.shape[0]
    for slot in range(slots):
        rows = pl.ds(slot * QROWS, QROWS)
        for index, ref in enumerate((m0, m1, m2, m3, m4)):

            @pl.when(code_ref[slot] == index)
            def _():
                pltpu.make_async_copy(ref.at[rows, :], msg.at[slot], sem.at[slot]).start()

    for slot in range(slots):
        rows = pl.ds(slot * QROWS, QROWS)
        pltpu.make_async_copy(m0.at[rows, :], msg.at[slot], sem.at[slot]).wait()
        stats = msg[slot, :, HEADS * HD:].astype(jnp.float32)
        own_stats = stat_ref[slot]
        for h in range(HEADS):
            cols = slice(h * HD, (h + 1) * HD)
            far = stats[:, 3 * h:3 * h + 1] + (
                stats[:, 3 * h + 1:3 * h + 2] + stats[:, 3 * h + 2:3 * h + 3]
            )
            near = own_stats[:, h:h + 1]
            top = jnp.maximum(far, near)
            far = jnp.exp2(far - top)
            near = jnp.exp2(near - top)
            scale = 1.0 / (far + near)
            out = (far * scale) * msg[slot, :, cols].astype(jnp.float32) + (
                near * scale
            ) * part_ref[slot, :, cols]
            out_ref[slot, :, cols] = out.astype(out_ref.dtype)


def merge_call(code, messages, own, shape):
    vmem = pl.BlockSpec(memory_space=pltpu.VMEM)
    anywhere = pl.BlockSpec(memory_space=pl.ANY)
    return pl.pallas_call(
        merge_kernel,
        in_specs=[pl.BlockSpec(memory_space=pltpu.SMEM)] + [anywhere] * 5 + [vmem] * 2,
        out_specs=vmem,
        out_shape=jax.ShapeDtypeStruct(shape, jnp.bfloat16),
        scratch_shapes=[
            pltpu.VMEM((shape[0], QROWS, MSG), jnp.bfloat16),
            pltpu.SemaphoreType.DMA((shape[0],)),
        ],
        name="merge",
    )(code, *messages, *own)


def live_bias(table_row, length, member, members):
    blocks = table_row.shape[0]
    per = blocks // members
    chunk = member ^ jnp.arange(members, dtype=jnp.int32)
    physical = chunk[:, None] * per + jnp.arange(per, dtype=jnp.int32)[None, :]
    logical = jnp.sum(
        jnp.where(
            table_row[None, None, :] == physical[:, :, None],
            jnp.arange(blocks, dtype=jnp.int32)[None, None, :],
            0,
        ),
        axis=2,
    )
    position = logical[:, :, None] * BLOCK + jnp.arange(BLOCK, dtype=jnp.int32)
    bias = jnp.where(position < length, 0.0, MASKED).astype(jnp.bfloat16)
    return bias.reshape(members, -1)


def shards(prompt_cache, queries, new_cache, offsets, lengths, block_table):
    groups = lax.axis_size("group")
    members = lax.axis_size("tensor")
    member = lax.axis_index("tensor")
    place = lax.axis_index("group") % ROW
    n_rows = groups // ROW

    def in_row(value, pairs):
        whole = [(r * ROW + a, r * ROW + b) for r in range(n_rows) for a, b in pairs]
        return lax.ppermute(value, "group", whole)

    def cross_row(value, pairs, step):
        whole = [
            (r * ROW + a, (r + step) % n_rows * ROW + b) for r in range(n_rows) for a, b in pairs
        ]
        return lax.ppermute(value, "group", whole)

    caps = queries.shape[0]
    last_row = caps * QROWS
    marks = jnp.repeat(offsets[0].astype(jnp.bfloat16), TAG // caps)
    tagged = jnp.concatenate(
        [
            queries.reshape(last_row, HEADS * HD),
            jnp.broadcast_to(marks[:, None], (TAG, HEADS * HD)),
        ],
        axis=0,
    )
    over = cross_row(tagged, [(0, 0), (1, 1), (2, 2)], -1)
    near = [in_row(tagged, [(i, i - k) for i in range(k, ROW)]) for k in range(1, REACH)]

    def slab(j):
        return lax.dynamic_slice_in_dim(prompt_cache, (member ^ j) * HD, HD, 2)

    def exchanged(j):
        value = slab(j)
        return lax.ppermute(value, "tensor", [(m, m ^ j) for m in range(members)])

    chunk = {j: exchanged(j) for j in range(1, members)}
    chunk[0] = slab(0)
    far = [in_row(over, [(i, ROW - k + i) for i in range(k)]) for k in range(1, REACH)]

    live = live_bias(block_table[0], lengths[0], member, members)
    biases = [
        jnp.broadcast_to(
            jnp.concatenate([live[j] for j in order])[:, None], (len(order) * live.shape[1], HD)
        )
        for order in ORDER
    ]
    q_all = jnp.stack(
        [tagged]
        + [jnp.where(place + k >= ROW, far[k - 1], near[k - 1]) for k in range(1, REACH)]
    )
    slots = REACH * caps
    asked = q_all[:, last_row::TAG // caps, 0].astype(jnp.int32)
    wanted = (asked == jnp.arange(REACH, dtype=jnp.int32)[:, None]).astype(jnp.int32).reshape(-1)
    code = jnp.where(place == 2, 3, jnp.where(asked[3] == 3, 0, asked[3]))
    pick = jnp.broadcast_to(jnp.repeat(code, QROWS)[:, None], (last_row, HD))
    source = jnp.where(offsets[0] <= place, offsets[0], REACH)
    own = own_call(queries, new_cache)
    q_all, wanted, own, pick, source, biases = lax.optimization_barrier(
        (q_all, wanted, own, pick, source, biases)
    )

    state = flash_call(wanted, biases[0], q_all, [chunk[j] for j in ORDER[0]], None, (0, slots), caps)
    state = flash_call(wanted, biases[1], q_all, [chunk[j] for j in ORDER[1]], state, (0, slots), caps)
    final = partial(flash_call, wanted, biases[2], q_all, [chunk[j] for j in ORDER[2]], state)
    message = [None, *final((caps, slots - caps), caps, True)]

    gathered = [
        in_row(message[1], [(7, 5)]),
        in_row(message[2], [(6, 5), (7, 6)]),
        in_row(message[3], [(7, 2)]),
    ]
    back = [in_row(message[k], [(i, i + k) for i in range(ROW - k)]) for k in range(1, REACH)]
    pick = pick[:, :1]
    passed = jnp.where(
        pick == 1,
        gathered[0],
        jnp.where(pick == 2, gathered[1], jnp.where(pick == 3, gathered[2], message[3])),
    )
    crossed = cross_row(passed, [(5, 0), (6, 1), (2, 2)], 1)
    (message[0],) = final((0, caps), caps, True)
    return merge_call(source, [message[0], *back, crossed], own, queries.shape)


def solution(mesh):
    in_specs = (
        P(None, ("group", "tensor"), None),
        P("group", None, "tensor"),
        P(None, "group", None, "tensor"),
        P("group", None),
        P("group"),
        P("group", None),
    )
    out_specs = P("group", None, "tensor")

    return jax.shard_map(shards, mesh=mesh, in_specs=in_specs, out_specs=out_specs, check_vma=False)
```

profile of v0, /device:TPU:161, one launch (start us, length us, event | category | flops | bytes accessed | tf_op | source)
XLA Modules:
  0.0 215.0 jit_solution(8624297084803586514)
XLA Ops:
  3.2 2.6 %collective-permute-start.2 = (bf16[144,1024]{1,0:T(8,128)(2,1)S(1)}, bf16[144,1024]{1,0:T(8,128)(2,1)S(1)}, u32[]{:S(2)}, u32[]{:S(2)}) collective-permute-start(bf16[144,1024]{1,0:T(8,128)(2,1)S(1)} %get-tuple-element.50), channel_id=1, source_target_pairs={{8,0},{16,8},{24,16},{32,24},{40,32},{48,40},{56,48},{72,64},{80,7... | collective-permute-start | bytes 884744 | tf_op jit(solution)/shard_map/ppermute | solution.py:265
  5.8 12.2 %collective-permute-start = (bf16[144,1024]{1,0:T(8,128)(2,1)S(1)}, bf16[144,1024]{1,0:T(8,128)(2,1)}, u32[]{:S(2)}, u32[]{:S(2)}) collective-permute-start(bf16[144,1024]{1,0:T(8,128)(2,1)S(1)} %get-tuple-element.50), channel_id=1, source_target_pairs={{0,448},{8,456},{16,464},{64,0},{72,8},{80,16},{128,64},{136,72},{... | collective-permute-start | bytes 884744 | tf_op jit(solution)/shard_map/ppermute | solution.py:271
  22.2 11.5 %collective-permute-done = bf16[144,1024]{1,0:T(8,128)(2,1)} collective-permute-done((bf16[144,1024]{1,0:T(8,128)(2,1)S(1)}, bf16[144,1024]{1,0:T(8,128)(2,1)}, u32[]{:S(2)}, u32[]{:S(2)}) %collective-permute-start) | collective-permute-done | bytes 294944 | tf_op jit(solution)/shard_map/ppermute | solution.py:271
  35.1 2.6 %constant_dynamic-slice_fusion = (bf16[2,512,128]{2,1,0:T(8,128)(2,1)}, bf16[2,512,128]{2,1,0:T(8,128)(2,1)}, bf16[2,512,128]{2,1,0:T(8,128)(2,1)}, bf16[2,512,1...) fusion(bf16[2,512,1024]{2,1,0:T(8,128)(2,1)} %param.6, ...), kind=kLoop, calls=%fused_computation.15 | loop fusion | bytes 4194336 | tf_op jit(solution)/shard_map/dynamic_slice | solution.py:287
  38.5 2.5 %own_part.1 = (f32[2,64,1024]{2,1,0:T(8,128)}, f32[2,64,128]{2,1,0:T(8,128)}) custom-call(bf16[2,64,1024]{2,1,0:T(8,128)(2,1)} %q_ref.1, bf16[2,2,64,128]{3,2,1,0:T(8,128)(2,1)} %new_ref.1), custom_call_target="tpu_custom_call" | custom-call | tf_op jit(solution)/shard_map/own_part/pallas_call | solution.py:181
  40.9 11.7 %collective-permute-start.13 = (bf16[2,512,128]{2,1,0:T(8,128)(2,1)}, bf16[2,512,128]{2,1,0:T(8,128)(2,1)}, u32[]{:S(2)}, u32[]{:S(2)}) collective-permute-start(bf16[2,512,128]{2,1,0:T(8,128)(2,1)} %get-tuple-element.41), channel_id=1, source_target_pairs={{0,5},{1,4},{2,7},{3,6},{4,1},{5,0},{6,3},{7,2},{8,13},{9,12},{10,... | collective-permute-start | bytes 786440 | tf_op jit(solution)/shard_map/ppermute | solution.py:291
  54.0 7.0 %collective-permute-start.11 = (bf16[2,512,128]{2,1,0:T(8,128)(2,1)}, bf16[2,512,128]{2,1,0:T(8,128)(2,1)}, u32[]{:S(2)}, u32[]{:S(2)}) collective-permute-start(bf16[2,512,128]{2,1,0:T(8,128)(2,1)} %get-tuple-element.42), channel_id=1, source_target_pairs={{0,4},{1,5},{2,6},{3,7},{4,0},{5,1},{6,2},{7,3},{8,12},{9,13},{10,... | collective-permute-start | bytes 786440 | tf_op jit(solution)/shard_map/ppermute | solution.py:291
  61.0 3.9 %collective-permute-start.10 = (bf16[2,512,128]{2,1,0:T(8,128)(2,1)S(1)}, bf16[2,512,128]{2,1,0:T(8,128)(2,1)}, u32[]{:S(2)}, u32[]{:S(2)}) collective-permute-start(bf16[2,512,128]{2,1,0:T(8,128)(2,1)S(1)} %get-tuple-element.44), channel_id=1, source_target_pairs={{0,3},{1,2},{2,1},{3,0},{4,7},{5,6},{6,5},{7,4},{8,11},{9,10},{10,... | collective-permute-start | bytes 786440 | tf_op jit(solution)/shard_map/ppermute | solution.py:291
  65.0 2.6 %collective-permute-start.9 = (bf16[2,512,128]{2,1,0:T(8,128)(2,1)S(1)}, bf16[2,512,128]{2,1,0:T(8,128)(2,1)S(1)}, u32[]{:S(2)}, u32[]{:S(2)}) collective-permute-start(bf16[2,512,128]{2,1,0:T(8,128)(2,1)S(1)} %get-tuple-element.45), channel_id=1, source_target_pairs={{0,6},{1,7},{2,4},{3,5},{4,2},{5,3},{6,0},{7,1},{8,14},{9,15},{10,... | collective-permute-start | bytes 786440 | tf_op jit(solution)/shard_map/ppermute | solution.py:291
  67.6 3.7 %collective-permute-start.12 = (bf16[2,512,128]{2,1,0:T(8,128)(2,1)S(1)}, bf16[2,512,128]{2,1,0:T(8,128)(2,1)S(1)}, u32[]{:S(2)}, u32[]{:S(2)}) collective-permute-start(bf16[2,512,128]{2,1,0:T(8,128)(2,1)S(1)} %get-tuple-element.48), channel_id=1, source_target_pairs={{0,1},{1,0},{2,3},{3,2},{4,5},{5,4},{6,7},{7,6},{8,9},{9,8},{10,11... | collective-permute-start | bytes 786440 | tf_op jit(solution)/shard_map/ppermute | solution.py:291
  75.6 13.7 %collective-permute-done.13.refs_3_ = bf16[2,512,128]{2,1,0:T(8,128)(2,1)} collective-permute-done((bf16[2,512,128]{2,1,0:T(8,128)(2,1)}, bf16[2,512,128]{2,1,0:T(8,128)(2,1)}, u32[]{:S(2)}, u32[]{:S(2)}) %collective-permute-start.13) | collective-permute-done | bytes 262176 | tf_op jit(solution)/shard_map/ppermute | solution.py:291
  89.3 6.3 %collective-permute-start.8 = (bf16[2,512,128]{2,1,0:T(8,128)(2,1)S(1)}, bf16[2,512,128]{2,1,0:T(8,128)(2,1)}, u32[]{:S(2)}, u32[]{:S(2)}) collective-permute-start(bf16[2,512,128]{2,1,0:T(8,128)(2,1)S(1)} %get-tuple-element.46), channel_id=1, source_target_pairs={{0,2},{1,3},{2,0},{3,1},{4,6},{5,7},{6,4},{7,5},{8,10},{9,11},{10,... | collective-permute-start | bytes 786440 | tf_op jit(solution)/shard_map/ppermute | solution.py:291
  95.6 1.3 collective-permute-done.11.refs_1_
  96.9 7.1 %collective-permute-start.7 = (bf16[2,512,128]{2,1,0:T(8,128)(2,1)S(1)}, bf16[2,512,128]{2,1,0:T(8,128)(2,1)S(1)}, u32[]{:S(2)}, u32[]{:S(2)}) collective-permute-start(bf16[2,512,128]{2,1,0:T(8,128)(2,1)S(1)} %get-tuple-element.47), channel_id=1, source_target_pairs={{0,7},{1,6},{2,5},{3,4},{4,3},{5,2},{6,1},{7,0},{8,15},{9,14},{10,... | collective-permute-start | bytes 786440 | tf_op jit(solution)/shard_map/ppermute | solution.py:291
  104.0 33.4 %collective-permute-done.12.refs_2_ = bf16[2,512,128]{2,1,0:T(8,128)(2,1)S(1)} collective-permute-done((bf16[2,512,128]{2,1,0:T(8,128)(2,1)S(1)}, bf16[2,512,128]{2,1,0:T(8,128)(2,1)S(1)}, u32[]{:S(2)}, u32[]{:S(2)}) %collective-permute-start.12) | collective-permute-done | bytes 262176 | tf_op jit(solution)/shard_map/ppermute | solution.py:291
  138.1 14.5 %flash_part.2 = (f32[8,512,256]{2,1,0:T(8,128)}, f32[8,512,128]{2,1,0:T(8,128)}) custom-call(s32[8]{0:T(128)} %compare_convert_fusion.wanted_ref, bf16[2048,128]{1,0:T(8,128)(2,1)} %broadcast_in_dim.115.bias_ref, bf16[4,144,1024]{2,1,0:T(8,128)(2,1)} %copy-done, bf16[2,512,128]{2,1,0:T(8,128)(2,1)} %get-tuple-element.43.refs_0_, ...), custom_call_target="tpu_custom_call" | custom-call | flops 8589934592 | bytes 1048576 | tf_op jit(solution)/shard_map/flash_part/pallas_call | solution.py:136
  153.3 14.4 %flash_part.3 = (f32[8,512,256]{2,1,0:T(8,128)}, f32[8,512,128]{2,1,0:T(8,128)}) custom-call(s32[8]{0:T(128)} %compare_convert_fusion.wanted_ref, bf16[1536,128]{1,0:T(8,128)(2,1)} %broadcast_in_dim.116.bias_ref, bf16[4,144,1024]{2,1,0:T(8,128)(2,1)} %copy-done, bf16[2,512,128]{2,1,0:T(8,128)(2,1)} %collective-permute-done.8.refs_0_, ...), custom_call_target="tpu_custom_call" | custom-call | flops 6442450944 | bytes 786432 | tf_op jit(solution)/shard_map/flash_part/pallas_call | solution.py:136
  168.4 7.6 %flash_last.3 = (bf16[128,1152]{1,0:T(8,128)(2,1)}, bf16[128,1152]{1,0:T(8,128)(2,1)}, bf16[128,1152]{1,0:T(8,128)(2,1)}) custom-call(s32[8]{0:T(128)} %compare_convert_fusion.wanted_ref, bf16[512,128]{1,0:T(8,128)(2,1)} %broadcast_in_dim.118.bias_ref, bf16[4,144,1024]{2,1,0:T(8,128)(2,1)} %copy-done, bf16[2,512,128]{2,1,0:T(8,128)(2,1)} %copy-done.1, ...), custom_call_target="tpu_custom_call" | custom-call | flops 1610612736 | bytes 262144 | tf_op jit(solution)/shard_map/flash_last/pallas_call | solution.py:136
  178.1 1.9 collective-permute-start.14
  185.1 4.9 %flash_last.2.m0 = bf16[128,1152]{1,0:T(8,128)(2,1)} custom-call(s32[8]{0:T(128)} %compare_convert_fusion.wanted_ref, bf16[512,128]{1,0:T(8,128)(2,1)} %broadcast_in_dim.118.bias_ref, bf16[4,144,1024]{2,1,0:T(8,128)(2,1)} %copy-done, bf16[2,512,128]{2,1,0:T(8,128)(2,1)} %copy-done.1, f32[8,512,256]{2,1,0:T(8,128)} %get-tuple-element.33.refs_1_, ...), custom_call_target="tpu_custom_call" | custom-call | flops 536870912 | bytes 262144 | tf_op jit(solution)/shard_map/flash_last/pallas_call | solution.py:136
  190.1 1.4 collective-permute-done.15.m2
  191.5 5.2 %collective-permute-done.16.m3 = bf16[128,1152]{1,0:T(8,128)(2,1)S(1)} collective-permute-done((bf16[128,1152]{1,0:T(8,128)(2,1)}, bf16[128,1152]{1,0:T(8,128)(2,1)S(1)}, u32[]{:S(2)}, u32[]{:S(2)}) %collective-permute-start.16) | collective-permute-done | bytes 294944 | tf_op jit(solution)/shard_map/ppermute | solution.py:265
  196.6 13.6 %collective-permute-done.20.m4 = bf16[128,1152]{1,0:T(8,128)(2,1)S(1)} collective-permute-done((bf16[128,1152]{1,0:T(8,128)(2,1)S(1)}, bf16[128,1152]{1,0:T(8,128)(2,1)S(1)}, u32[]{:S(2)}, u32[]{:S(2)}) %collective-permute-start.20) | collective-permute-done | bytes 294944 | tf_op jit(solution)/shard_map/ppermute | solution.py:271
  211.0 4.0 %merge.1 = bf16[2,64,1024]{2,1,0:T(8,128)(2,1)} custom-call(s32[2]{0:T(128)} %compare_select_fusion.code_ref, bf16[128,1152]{1,0:T(8,128)(2,1)} %flash_last.2.m0, bf16[128,1152]{1,0:T(8,128)(2,1)} %copy-done.2, bf16[128,1152]{1,0:T(8,128)(2,1)} %copy-done.3, bf16[128,1152]{1,0:T(8,128)(2,1)} %copy-done.4, bf16[128,1152]{1,0:T(8,128)(2,1)} %copy-done.5, ...), custom_call_target="tpu_custom_call" | custom-call | tf_op jit(solution)/shard_map/merge/pallas_call | solution.py:225
  (76 shorter events, 24.4 us)
Async XLA Ops:
  1.9 39.0 %collective-permute-start.4 = (bf16[144,1024]{1,0:T(8,128)(2,1)S(1)}, bf16[144,1024]{1,0:T(8,128)(2,1)S(1)}, u32[]{:S(2)}, u32[]{:S(2)}) collective-permute-start(bf16[144,1024]{1,0:T(8,128)(2,1)S(1)} %get-tuple-element.50), channel_id=1, source_target_pairs={{16,0},{24,8},{32,16},{40,24},{48,32},{56,40},{80,64},{88,72},{96,... | collective-permute-start | bytes 884744 | tf_op jit(solution)/shard_map/ppermute | solution.py:265
  3.2 50.8 %collective-permute-start.2 = (bf16[144,1024]{1,0:T(8,128)(2,1)S(1)}, bf16[144,1024]{1,0:T(8,128)(2,1)S(1)}, u32[]{:S(2)}, u32[]{:S(2)}) collective-permute-start(bf16[144,1024]{1,0:T(8,128)(2,1)S(1)} %get-tuple-element.50), channel_id=1, source_target_pairs={{8,0},{16,8},{24,16},{32,24},{40,32},{48,40},{56,48},{72,64},{80,7... | collective-permute-start | bytes 884744 | tf_op jit(solution)/shard_map/ppermute | solution.py:265
  5.8 28.0 %collective-permute-start = (bf16[144,1024]{1,0:T(8,128)(2,1)S(1)}, bf16[144,1024]{1,0:T(8,128)(2,1)}, u32[]{:S(2)}, u32[]{:S(2)}) collective-permute-start(bf16[144,1024]{1,0:T(8,128)(2,1)S(1)} %get-tuple-element.50), channel_id=1, source_target_pairs={{0,448},{8,456},{16,464},{64,0},{72,8},{80,16},{128,64},{136,72},{... | collective-permute-start | bytes 884744 | tf_op jit(solution)/shard_map/ppermute | solution.py:271
  18.0 47.0 %collective-permute-start.6 = (bf16[144,1024]{1,0:T(8,128)(2,1)S(1)}, bf16[144,1024]{1,0:T(8,128)(2,1)S(1)}, u32[]{:S(2)}, u32[]{:S(2)}) collective-permute-start(bf16[144,1024]{1,0:T(8,128)(2,1)S(1)} %get-tuple-element.50), channel_id=1, source_target_pairs={{24,0},{32,8},{40,16},{48,24},{56,32},{88,64},{96,72},{104,80},{11... | collective-permute-start | bytes 884744 | tf_op jit(solution)/shard_map/ppermute | solution.py:265
  33.8 18.9 %collective-permute-start.3 = (bf16[144,1024]{1,0:T(8,128)(2,1)}, bf16[144,1024]{1,0:T(8,128)(2,1)S(1)}, u32[]{:S(2)}, u32[]{:S(2)}) collective-permute-start(bf16[144,1024]{1,0:T(8,128)(2,1)} %collective-permute-done), channel_id=1, source_target_pairs={{0,48},{8,56},{64,112},{72,120},{128,176},{136,184},{192,240},{200... | collective-permute-start | bytes 884744 | tf_op jit(solution)/shard_map/ppermute | solution.py:265
  37.7 23.3 %collective-permute-start.1 = (bf16[144,1024]{1,0:T(8,128)(2,1)}, bf16[144,1024]{1,0:T(8,128)(2,1)S(1)}, u32[]{:S(2)}, u32[]{:S(2)}) collective-permute-start(bf16[144,1024]{1,0:T(8,128)(2,1)} %collective-permute-done), channel_id=1, source_target_pairs={{0,56},{64,120},{128,184},{192,248},{256,312},{320,376},{384,440},... | collective-permute-start | bytes 884744 | tf_op jit(solution)/shard_map/ppermute | solution.py:265
  40.9 48.3 %collective-permute-start.13 = (bf16[2,512,128]{2,1,0:T(8,128)(2,1)}, bf16[2,512,128]{2,1,0:T(8,128)(2,1)}, u32[]{:S(2)}, u32[]{:S(2)}) collective-permute-start(bf16[2,512,128]{2,1,0:T(8,128)(2,1)} %get-tuple-element.41), channel_id=1, source_target_pairs={{0,5},{1,4},{2,7},{3,6},{4,1},{5,0},{6,3},{7,2},{8,13},{9,12},{10,... | collective-permute-start | bytes 786440 | tf_op jit(solution)/shard_map/ppermute | solution.py:291
  52.6 14.9 %collective-permute-start.5 = (bf16[144,1024]{1,0:T(8,128)(2,1)}, bf16[144,1024]{1,0:T(8,128)(2,1)S(1)}, u32[]{:S(2)}, u32[]{:S(2)}) collective-permute-start(bf16[144,1024]{1,0:T(8,128)(2,1)} %collective-permute-done), channel_id=1, source_target_pairs={{0,40},{8,48},{16,56},{64,104},{72,112},{80,120},{128,168},{136,17... | collective-permute-start | bytes 884744 | tf_op jit(solution)/shard_map/ppermute | solution.py:265
  54.0 42.9 %collective-permute-start.11 = (bf16[2,512,128]{2,1,0:T(8,128)(2,1)}, bf16[2,512,128]{2,1,0:T(8,128)(2,1)}, u32[]{:S(2)}, u32[]{:S(2)}) collective-permute-start(bf16[2,512,128]{2,1,0:T(8,128)(2,1)} %get-tuple-element.42), channel_id=1, source_target_pairs={{0,4},{1,5},{2,6},{3,7},{4,0},{5,1},{6,2},{7,3},{8,12},{9,13},{10,... | collective-permute-start | bytes 786440 | tf_op jit(solution)/shard_map/ppermute | solution.py:291
  61.0 91.6 %collective-permute-start.10 = (bf16[2,512,128]{2,1,0:T(8,128)(2,1)S(1)}, bf16[2,512,128]{2,1,0:T(8,128)(2,1)}, u32[]{:S(2)}, u32[]{:S(2)}) collective-permute-start(bf16[2,512,128]{2,1,0:T(8,128)(2,1)S(1)} %get-tuple-element.44), channel_id=1, source_target_pairs={{0,3},{1,2},{2,1},{3,0},{4,7},{5,6},{6,5},{7,4},{8,11},{9,10},{10,... | collective-permute-start | bytes 786440 | tf_op jit(solution)/shard_map/ppermute | solution.py:291
  65.0 87.6 %collective-permute-start.9 = (bf16[2,512,128]{2,1,0:T(8,128)(2,1)S(1)}, bf16[2,512,128]{2,1,0:T(8,128)(2,1)S(1)}, u32[]{:S(2)}, u32[]{:S(2)}) collective-permute-start(bf16[2,512,128]{2,1,0:T(8,128)(2,1)S(1)} %get-tuple-element.45), channel_id=1, source_target_pairs={{0,6},{1,7},{2,4},{3,5},{4,2},{5,3},{6,0},{7,1},{8,14},{9,15},{10,... | collective-permute-start | bytes 786440 | tf_op jit(solution)/shard_map/ppermute | solution.py:291
  67.6 69.8 %collective-permute-start.12 = (bf16[2,512,128]{2,1,0:T(8,128)(2,1)S(1)}, bf16[2,512,128]{2,1,0:T(8,128)(2,1)S(1)}, u32[]{:S(2)}, u32[]{:S(2)}) collective-permute-start(bf16[2,512,128]{2,1,0:T(8,128)(2,1)S(1)} %get-tuple-element.48), channel_id=1, source_target_pairs={{0,1},{1,0},{2,3},{3,2},{4,5},{5,4},{6,7},{7,6},{8,9},{9,8},{10,11... | collective-permute-start | bytes 786440 | tf_op jit(solution)/shard_map/ppermute | solution.py:291
  71.5 65.9 %copy-start = (bf16[4,144,1024]{2,1,0:T(8,128)(2,1)}, bf16[4,144,1024]{2,1,0:T(8,128)(2,1)S(1)}, u32[]{:S(2)}) copy-start(bf16[4,144,1024]{2,1,0:T(8,128)(2,1)S(1)} %pad_maximum_fusion.q_ref) | copy-start | bytes 3538948
  89.3 63.3 %collective-permute-start.8 = (bf16[2,512,128]{2,1,0:T(8,128)(2,1)S(1)}, bf16[2,512,128]{2,1,0:T(8,128)(2,1)}, u32[]{:S(2)}, u32[]{:S(2)}) collective-permute-start(bf16[2,512,128]{2,1,0:T(8,128)(2,1)S(1)} %get-tuple-element.46), channel_id=1, source_target_pairs={{0,2},{1,3},{2,0},{3,1},{4,6},{5,7},{6,4},{7,5},{8,10},{9,11},{10,... | collective-permute-start | bytes 786440 | tf_op jit(solution)/shard_map/ppermute | solution.py:291
  96.9 70.8 %collective-permute-start.7 = (bf16[2,512,128]{2,1,0:T(8,128)(2,1)S(1)}, bf16[2,512,128]{2,1,0:T(8,128)(2,1)S(1)}, u32[]{:S(2)}, u32[]{:S(2)}) collective-permute-start(bf16[2,512,128]{2,1,0:T(8,128)(2,1)S(1)} %get-tuple-element.47), channel_id=1, source_target_pairs={{0,7},{1,6},{2,5},{3,4},{4,3},{5,2},{6,1},{7,0},{8,15},{9,14},{10,... | collective-permute-start | bytes 786440 | tf_op jit(solution)/shard_map/ppermute | solution.py:291
  176.1 5.3 %collective-permute-start.17 = (bf16[128,1152]{1,0:T(8,128)(2,1)}, bf16[128,1152]{1,0:T(8,128)(2,1)S(1)}, u32[]{:S(2)}, u32[]{:S(2)}) collective-permute-start(bf16[128,1152]{1,0:T(8,128)(2,1)} %get-tuple-element.35), channel_id=1, source_target_pairs={{56,40},{120,104},{184,168},{248,232},{312,296},{376,360},{440,424... | collective-permute-start | bytes 884744 | tf_op jit(solution)/shard_map/ppermute | solution.py:265
  176.7 6.0 %collective-permute-start.18 = (bf16[128,1152]{1,0:T(8,128)(2,1)}, bf16[128,1152]{1,0:T(8,128)(2,1)S(1)}, u32[]{:S(2)}, u32[]{:S(2)}) collective-permute-start(bf16[128,1152]{1,0:T(8,128)(2,1)} %get-tuple-element.36), channel_id=1, source_target_pairs={{48,40},{56,48},{112,104},{120,112},{176,168},{184,176},{240,232},... | collective-permute-start | bytes 884744 | tf_op jit(solution)/shard_map/ppermute | solution.py:265
  177.4 5.3 %collective-permute-start.19 = (bf16[128,1152]{1,0:T(8,128)(2,1)}, bf16[128,1152]{1,0:T(8,128)(2,1)S(1)}, u32[]{:S(2)}, u32[]{:S(2)}) collective-permute-start(bf16[128,1152]{1,0:T(8,128)(2,1)} %get-tuple-element.37), channel_id=1, source_target_pairs={{56,16},{120,80},{184,144},{248,208},{312,272},{376,336},{440,400}... | collective-permute-start | bytes 884744 | tf_op jit(solution)/shard_map/ppermute | solution.py:265
  178.1 12.0 %collective-permute-start.14 = (bf16[128,1152]{1,0:T(8,128)(2,1)}, bf16[128,1152]{1,0:T(8,128)(2,1)S(1)}, u32[]{:S(2)}, u32[]{:S(2)}) collective-permute-start(bf16[128,1152]{1,0:T(8,128)(2,1)} %get-tuple-element.35), channel_id=1, source_target_pairs={{0,8},{8,16},{16,24},{24,32},{32,40},{40,48},{48,56},{64,72},{72,8... | collective-permute-start | bytes 884744 | tf_op jit(solution)/shard_map/ppermute | solution.py:265
  180.0 11.4 %collective-permute-start.15 = (bf16[128,1152]{1,0:T(8,128)(2,1)}, bf16[128,1152]{1,0:T(8,128)(2,1)S(1)}, u32[]{:S(2)}, u32[]{:S(2)}) collective-permute-start(bf16[128,1152]{1,0:T(8,128)(2,1)} %get-tuple-element.36), channel_id=1, source_target_pairs={{0,16},{8,24},{16,32},{24,40},{32,48},{40,56},{64,80},{72,88},{80,... | collective-permute-start | bytes 884744 | tf_op jit(solution)/shard_map/ppermute | solution.py:265
  181.4 15.3 %collective-permute-start.16 = (bf16[128,1152]{1,0:T(8,128)(2,1)}, bf16[128,1152]{1,0:T(8,128)(2,1)S(1)}, u32[]{:S(2)}, u32[]{:S(2)}) collective-permute-start(bf16[128,1152]{1,0:T(8,128)(2,1)} %get-tuple-element.37), channel_id=1, source_target_pairs={{0,24},{8,32},{16,40},{24,48},{32,56},{64,88},{72,96},{80,104},{88... | collective-permute-start | bytes 884744 | tf_op jit(solution)/shard_map/ppermute | solution.py:265
  183.8 26.4 %collective-permute-start.20 = (bf16[128,1152]{1,0:T(8,128)(2,1)S(1)}, bf16[128,1152]{1,0:T(8,128)(2,1)S(1)}, u32[]{:S(2)}, u32[]{:S(2)}) collective-permute-start(bf16[128,1152]{1,0:T(8,128)(2,1)S(1)} %select_select_fusion), channel_id=1, source_target_pairs={{40,64},{48,72},{16,80},{104,128},{112,136},{80,144},{168,192},{17... | collective-permute-start | bytes 884744 | tf_op jit(solution)/shard_map/ppermute | solution.py:271
  190.1 20.2 %copy-start.2 = (bf16[128,1152]{1,0:T(8,128)(2,1)}, bf16[128,1152]{1,0:T(8,128)(2,1)S(1)}, u32[]{:S(2)}) copy-start(bf16[128,1152]{1,0:T(8,128)(2,1)S(1)} %collective-permute-done.14.m1) | copy-start | bytes 884740
  191.5 18.8 %copy-start.3 = (bf16[128,1152]{1,0:T(8,128)(2,1)}, bf16[128,1152]{1,0:T(8,128)(2,1)S(1)}, u32[]{:S(2)}) copy-start(bf16[128,1152]{1,0:T(8,128)(2,1)S(1)} %collective-permute-done.15.m2) | copy-start | bytes 884740
  (5 other events, 16.5 us)
where the time goes:
time: 216 us; the launch traced here: 215 us
  waiting for transfers between devices  80.2 us (37%)
  starting transfers between devices  70.7 us (33%)
  Pallas kernels  47.9 us (22%)
  local copies, waits for them, and re-layouts  8.99 us (4%)
  other arithmetic  6.11 us (3%)
    ppermute x7, waiting for transfers between devices, exchanged(): return lax.ppermute(value, 'tensor', [(m, m ^ j) for m in range(members)])  48.4 us
    ppermute x7, starting transfers between devices, exchanged(): return lax.ppermute(value, 'tensor', [(m, m ^ j) for m in range(members)])  42.2 us
    pallas_call x4, Pallas kernels, flash_call(): pl.pallas_call(partial(flash_kernel, n, lo, first, caps if last else None...  41.5 us
    ppermute x2, waiting for transfers between devices, cross_row(): return lax.ppermute(value, 'group', whole)  25.2 us
    ppermute x12, starting transfers between devices, in_row(): return lax.ppermute(value, 'group', whole)  15 us
    ppermute x2, starting transfers between devices, cross_row(): return lax.ppermute(value, 'group', whole)  13.5 us
    ppermute x12, waiting for transfers between devices, in_row(): return lax.ppermute(value, 'group', whole)  6.6 us
  transfers between devices with their start and end apart: 21, of which 7 were waited for; matrix products, arithmetic and copies ran while one was open for 5% of the time, Pallas kernels for 17%

commit v1 on v0

--- a/solution.py
+++ b/solution.py
@@ -13,13 +13,12 @@
 STEPS = 4
 REACH = 4
 ROW = 8
-TAG = 16
 PART = 4
 HEADS = 8
 QROWS = 64
 MSG = HEADS * HD + 128
 MASKED = -1e30
-ORDER = ((0, 4, 1, 5), (2, 6, 3), (7,))
+ORDER = ((0, 1, 2, 3), (4, 5, 6), (7,))
 SCALE2 = 1.4426950408889634 * HD ** (-0.5)
 
 
@@ -39,7 +38,7 @@
 
 
 def flash_kernel(n_chunks, lo, first, outs_of, wanted_ref, bias_ref, q_ref, *refs):
-    k_wide, v_wide = refs[-2:]
+    k_all, v_wide = refs[-2:]
     kv_refs = refs[:n_chunks]
     refs = refs[n_chunks:-2]
     if first:
@@ -54,16 +53,14 @@
     def _():
         for m in range(n_chunks):
             rows = slice(m * tokens, (m + 1) * tokens)
-            k_wide[rows, :HD] = kv_refs[m][0]
+            k_all[rows, :] = kv_refs[m][0]
             v_wide[rows, :HD] = kv_refs[m][1]
-        k_wide[:, HD:] = bias_ref[...]
         v_wide[:, HD:] = jnp.ones((n_chunks * tokens, HD), jnp.bfloat16)
 
     @pl.when(wanted_ref[lo + step] == 1)
     def _():
         lane = lax.broadcasted_iota(jnp.int32, (1, HD), 1)
         count = PART * QROWS
-        mark = jnp.broadcast_to(jnp.where(lane == 0, 1.0, 0.0).astype(jnp.bfloat16), (count, HD))
         parts = []
         stats = jnp.zeros((QROWS, HD), jnp.float32)
         for block in range(HEADS // PART):
@@ -71,11 +68,11 @@
             heads = range(block * PART, (block + 1) * PART)
             q = jnp.concatenate([q_ref[0, :, h * HD:(h + 1) * HD] for h in heads], axis=0)
             s = lax.dot_general(
-                jnp.concatenate([q, mark], axis=1),
-                k_wide[...],
+                q,
+                k_all[...],
                 (((1,), (1,)), ((), ())),
                 preferred_element_type=jnp.float32,
-            )
+            ) + bias_ref[...]
             top = jnp.broadcast_to(jnp.max(s, axis=1, keepdims=True), (count, HD))
             if not first:
                 old = top_in[0, rows]
@@ -94,7 +91,7 @@
             for index, h in enumerate(heads):
                 mine = slice(index * QROWS, (index + 1) * QROWS)
                 for c in range(3):
-                    stats = jnp.where(lane == 3 * h + c, big[c][mine], stats)
+                    stats = jnp.where(lane == c * HEADS + h, big[c][mine], stats)
         if outs_of is None:
             return
         for index, msg in enumerate(outs):
@@ -140,7 +137,10 @@
             grid=(count,),
             in_specs=in_specs,
             out_specs=out_specs,
-            scratch_shapes=[pltpu.VMEM((tokens, 2 * HD), jnp.bfloat16)] * 2,
+            scratch_shapes=[
+                pltpu.VMEM((tokens, HD), jnp.bfloat16),
+                pltpu.VMEM((tokens, 2 * HD), jnp.bfloat16),
+            ],
         ),
         out_shape=out_shape,
         compiler_params=pltpu.CompilerParams(dimension_semantics=("arbitrary",)),
@@ -202,26 +202,27 @@
         rows = pl.ds(slot * QROWS, QROWS)
         pltpu.make_async_copy(m0.at[rows, :], msg.at[slot], sem.at[slot]).wait()
         stats = msg[slot, :, HEADS * HD:].astype(jnp.float32)
-        own_stats = stat_ref[slot]
+        far = stats + (
+            pltpu.roll(stats, HD - HEADS, 1) + pltpu.roll(stats, HD - 2 * HEADS, 1)
+        )
+        near = stat_ref[slot]
+        top = jnp.maximum(far, near)
+        far = jnp.exp2(far - top)
+        near = jnp.exp2(near - top)
+        scale = 1.0 / (far + near)
+        far = far * scale
+        near = near * scale
         for h in range(HEADS):
             cols = slice(h * HD, (h + 1) * HD)
-            far = stats[:, 3 * h:3 * h + 1] + (
-                stats[:, 3 * h + 1:3 * h + 2] + stats[:, 3 * h + 2:3 * h + 3]
+            out = far[:, h:h + 1] * msg[slot, :, cols].astype(jnp.float32) + (
+                near[:, h:h + 1] * part_ref[slot, :, cols]
             )
-            near = own_stats[:, h:h + 1]
-            top = jnp.maximum(far, near)
-            far = jnp.exp2(far - top)
-            near = jnp.exp2(near - top)
-            scale = 1.0 / (far + near)
-            out = (far * scale) * msg[slot, :, cols].astype(jnp.float32) + (
-                near * scale
-            ) * part_ref[slot, :, cols]
             out_ref[slot, :, cols] = out.astype(out_ref.dtype)
 
 
 def merge_call(code, messages, own, shape):
     vmem = pl.BlockSpec(memory_space=pltpu.VMEM)
-    anywhere = pl.BlockSpec(memory_space=pl.ANY)
+    anywhere = pl.BlockSpec(memory_space=pltpu.HBM)
     return pl.pallas_call(
         merge_kernel,
         in_specs=[pl.BlockSpec(memory_space=pltpu.SMEM)] + [anywhere] * 5 + [vmem] * 2,
@@ -249,7 +250,7 @@
         axis=2,
     )
     position = logical[:, :, None] * BLOCK + jnp.arange(BLOCK, dtype=jnp.int32)
-    bias = jnp.where(position < length, 0.0, MASKED).astype(jnp.bfloat16)
+    bias = jnp.where(position < length, 0.0, MASKED).astype(jnp.float32)
     return bias.reshape(members, -1)
 
 
@@ -272,16 +273,13 @@
 
     caps = queries.shape[0]
     last_row = caps * QROWS
-    marks = jnp.repeat(offsets[0].astype(jnp.bfloat16), TAG // caps)
-    tagged = jnp.concatenate(
-        [
-            queries.reshape(last_row, HEADS * HD),
-            jnp.broadcast_to(marks[:, None], (TAG, HEADS * HD)),
-        ],
-        axis=0,
-    )
-    over = cross_row(tagged, [(0, 0), (1, 1), (2, 2)], -1)
-    near = [in_row(tagged, [(i, i - k) for i in range(k, ROW)]) for k in range(1, REACH)]
+    flat_q = queries.reshape(last_row, HEADS * HD)
+    hop = in_row(flat_q, [(1, 5)])
+    over = cross_row(jnp.where(place == 5, hop, flat_q), [(0, 0), (5, 5), (2, 2)], -1)
+    inside = [[(i, i - k) for i in range(k, ROW)] for k in range(1, REACH)]
+    tags = [in_row(offsets, inside[k - 1]) for k in range(1, REACH)]
+    far_offsets = cross_row(offsets, [(0, 5), (1, 6)], -1)
+    near = [in_row(flat_q, [(i, i - k) for i in range(k, ROW)]) for k in range(1, REACH)]
 
     def slab(j):
         return lax.dynamic_slice_in_dim(prompt_cache, (member ^ j) * HD, HD, 2)
@@ -292,31 +290,26 @@
 
     chunk = {j: exchanged(j) for j in range(1, members)}
     chunk[0] = slab(0)
-    far = [in_row(over, [(i, ROW - k + i) for i in range(k)]) for k in range(1, REACH)]
+    far = [in_row(over, [((0, 5, 2)[i], ROW - k + i) for i in range(k)]) for k in range(1, REACH)]
 
     live = live_bias(block_table[0], lengths[0], member, members)
-    biases = [
-        jnp.broadcast_to(
-            jnp.concatenate([live[j] for j in order])[:, None], (len(order) * live.shape[1], HD)
-        )
-        for order in ORDER
-    ]
-    q_all = jnp.stack(
-        [tagged]
-        + [jnp.where(place + k >= ROW, far[k - 1], near[k - 1]) for k in range(1, REACH)]
-    )
+    biases = [jnp.concatenate([live[j] for j in order])[None, :] for order in ORDER]
     slots = REACH * caps
-    asked = q_all[:, last_row::TAG // caps, 0].astype(jnp.int32)
-    wanted = (asked == jnp.arange(REACH, dtype=jnp.int32)[:, None]).astype(jnp.int32).reshape(-1)
-    code = jnp.where(place == 2, 3, jnp.where(asked[3] == 3, 0, asked[3]))
+    outside = [place + k >= ROW for k in range(1, REACH)]
+    wanted = jnp.concatenate(
+        [offsets[0] == 0] + [o | (t[0] == k) for k, (o, t) in enumerate(zip(outside, tags), 1)]
+    ).astype(jnp.int32)
+    q_all = jnp.stack([flat_q] + [jnp.where(o, f, n) for o, f, n in zip(outside, far, near)])
+    q_all, wanted, biases = lax.optimization_barrier((q_all, wanted, biases))
+
+    state = flash_call(wanted, biases[0], q_all, [chunk[j] for j in ORDER[0]], None, (0, slots), caps)
+    state, later = lax.optimization_barrier((state, (queries, new_cache, far_offsets, offsets)))
+    own = own_call(*later[:2])
+    asked = later[2][0]
+    code = jnp.where(place == 2, 3, jnp.where(asked == 3, 0, asked))
     pick = jnp.broadcast_to(jnp.repeat(code, QROWS)[:, None], (last_row, HD))
-    source = jnp.where(offsets[0] <= place, offsets[0], REACH)
-    own = own_call(queries, new_cache)
-    q_all, wanted, own, pick, source, biases = lax.optimization_barrier(
-        (q_all, wanted, own, pick, source, biases)
-    )
-
-    state = flash_call(wanted, biases[0], q_all, [chunk[j] for j in ORDER[0]], None, (0, slots), caps)
+    source = jnp.where(later[3][0] <= place, later[3][0], REACH)
+    state, own, pick, source = lax.optimization_barrier((state, own, pick, source))
     state = flash_call(wanted, biases[1], q_all, [chunk[j] for j in ORDER[1]], state, (0, slots), caps)
     final = partial(flash_call, wanted, biases[2], q_all, [chunk[j] for j in ORDER[2]], state)
     message = [None, *final((caps, slots - caps), caps, True)]

time: 216 us -> 239 us (1.11)
  the two profiles are of different devices: /device:TPU:161 before, /device:TPU:33 now
where the time goes in v1:
time: 239 us; the launch traced here: 238 us
  starting transfers between devices  104 us (44%)
  waiting for transfers between devices  75.3 us (32%)
  Pallas kernels  46.5 us (19%)
  local copies, waits for them, and re-layouts  6.07 us (3%)
  other arithmetic  5.16 us (2%)
    ppermute x7, waiting for transfers between devices, exchanged(): return lax.ppermute(value, 'tensor', [(m, m ^ j) for m in range(members)])  54.7 us
    ppermute x16, starting transfers between devices, in_row(): return lax.ppermute(value, 'group', whole)  50.7 us
    pallas_call x4, Pallas kernels, flash_call(): pl.pallas_call(partial(flash_kernel, n, lo, first, caps if last else None...  40.8 us
    ppermute x7, starting transfers between devices, exchanged(): return lax.ppermute(value, 'tensor', [(m, m ^ j) for m in range(members)])  29.7 us
    ppermute x3, starting transfers between devices, cross_row(): return lax.ppermute(value, 'group', whole)  23.6 us
    ppermute x3, waiting for transfers between devices, cross_row(): return lax.ppermute(value, 'group', whole)  14.7 us
    ppermute x16, waiting for transfers between devices, in_row(): return lax.ppermute(value, 'group', whole)  5.9 us
  transfers between devices with their start and end apart: 26, of which 6 were waited for; matrix products, arithmetic and copies ran while one was open for 4% of the time, Pallas kernels for 15%

profile of v1, /device:TPU:33, one launch (start us, length us, event | category | flops | bytes accessed | tf_op | source)
XLA Modules:
  0.0 238.3 jit_solution(298221066424024613)
XLA Ops:
  2.6 2.6 %collective-permute-start.8 = (s32[1,2]{1,0:T(1,128)}, s32[1,2]{1,0:T(1,128)S(1)}, u32[]{:S(2)}, u32[]{:S(2)}) collective-permute-start(s32[1,2]{1,0:T(1,128)} %param.9), channel_id=1, source_target_pairs={{8,0},{16,8},{24,16},{32,24},{40,32},{48,40},{56,48},{72,64},{80,7... | collective-permute-start | bytes 32 | tf_op jit(solution)/shard_map/ppermute | solution.py:266
  5.2 21.6 %collective-permute-start.14 = (s32[1,2]{1,0:T(1,128)}, s32[1,2]{1,0:T(1,128)S(1)}, u32[]{:S(2)}, u32[]{:S(2)}) collective-permute-start(s32[1,2]{1,0:T(1,128)} %param.9), channel_id=1, source_target_pairs={{0,488},{8,496},{64,40},{72,48},{128,104},{136,112},{192,168},{200... | collective-permute-start | bytes 32 | tf_op jit(solution)/shard_map/ppermute | solution.py:272
  30.5 2.5 %constant_dynamic-slice_fusion.7 = (bf16[2,512,128]{2,1,0:T(8,128)(2,1)S(1)}, bf16[2,512,128]{2,1,0:T(8,128)(2,1)S(1)}, bf16[2,512,128]{2,1,0:T(8,128)(2,1)S(1)}...) fusion(bf16[2,512,1024]{2,1,0:T(8,128)(2,1)} %param.6, ...), kind=kLoop, calls=%fused_computation.28 | loop fusion | bytes 4194336 | tf_op jit(solution)/shard_map/dynamic_slice | solution.py:285
  39.6 5.9 %collective-permute-done.7 = bf16[128,1024]{1,0:T(8,128)(2,1)S(1)} collective-permute-done((bf16[128,1024]{1,0:T(8,128)(2,1)S(1)}, bf16[128,1024]{1,0:T(8,128)(2,1)S(1)}, u32[]{:S(2)}, u32[]{:S(2)}) %collective-permute-start.7) | collective-permute-done | bytes 262176 | tf_op jit(solution)/shard_map/ppermute | solution.py:266
  45.5 22.1 %collective-permute-start.3 = (bf16[128,1024]{1,0:T(8,128)(2,1)S(1)}, bf16[128,1024]{1,0:T(8,128)(2,1)S(1)}, u32[]{:S(2)}, u32[]{:S(2)}) collective-permute-start(bf16[128,1024]{1,0:T(8,128)(2,1)S(1)} %bitcast.49), channel_id=1, source_target_pairs={{8,0},{16,8},{24,16},{32,24},{40,32},{48,40},{56,48},{72,64},{80,7... | collective-permute-start | bytes 786440 | tf_op jit(solution)/shard_map/ppermute | solution.py:266
  68.4 1.9 collective-permute-start.18
  70.3 1.9 collective-permute-start.13
  72.3 7.7 %collective-permute-start.12 = (bf16[2,512,128]{2,1,0:T(8,128)(2,1)S(1)}, bf16[2,512,128]{2,1,0:T(8,128)(2,1)S(1)}, u32[]{:S(2)}, u32[]{:S(2)}) collective-permute-start(bf16[2,512,128]{2,1,0:T(8,128)(2,1)S(1)} %get-tuple-element.61), channel_id=1, source_target_pairs={{0,2},{1,3},{2,0},{3,1},{4,6},{5,7},{6,4},{7,5},{8,10},{9,11},{10,... | collective-permute-start | bytes 786440 | tf_op jit(solution)/shard_map/ppermute | solution.py:289
  80.0 1.9 collective-permute-start.11
  83.1 12.2 %collective-permute-done.13.refs_3_ = bf16[2,512,128]{2,1,0:T(8,128)(2,1)S(1)} collective-permute-done((bf16[2,512,128]{2,1,0:T(8,128)(2,1)S(1)}, bf16[2,512,128]{2,1,0:T(8,128)(2,1)S(1)}, u32[]{:S(2)}, u32[]{:S(2)}) %collective-permute-start.13) | collective-permute-done | bytes 262176 | tf_op jit(solution)/shard_map/ppermute | solution.py:289
  95.4 6.7 %collective-permute-start.16 = (bf16[2,512,128]{2,1,0:T(8,128)(2,1)S(1)}, bf16[2,512,128]{2,1,0:T(8,128)(2,1)S(1)}, u32[]{:S(2)}, u32[]{:S(2)}) collective-permute-start(bf16[2,512,128]{2,1,0:T(8,128)(2,1)S(1)} %get-tuple-element.58), channel_id=1, source_target_pairs={{0,4},{1,5},{2,6},{3,7},{4,0},{5,1},{6,2},{7,3},{8,12},{9,13},{10,... | collective-permute-start | bytes 786440 | tf_op jit(solution)/shard_map/ppermute | solution.py:289
  102.1 4.4 %collective-permute-done.12.refs_2_ = bf16[2,512,128]{2,1,0:T(8,128)(2,1)S(1)} collective-permute-done((bf16[2,512,128]{2,1,0:T(8,128)(2,1)S(1)}, bf16[2,512,128]{2,1,0:T(8,128)(2,1)S(1)}, u32[]{:S(2)}, u32[]{:S(2)}) %collective-permute-start.12) | collective-permute-done | bytes 262176 | tf_op jit(solution)/shard_map/ppermute | solution.py:289
  106.5 6.1 %collective-permute-start.15 = (bf16[2,512,128]{2,1,0:T(8,128)(2,1)S(1)}, bf16[2,512,128]{2,1,0:T(8,128)(2,1)S(1)}, u32[]{:S(2)}, u32[]{:S(2)}) collective-permute-start(bf16[2,512,128]{2,1,0:T(8,128)(2,1)S(1)} %get-tuple-element.59), channel_id=1, source_target_pairs={{0,7},{1,6},{2,5},{3,4},{4,3},{5,2},{6,1},{7,0},{8,15},{9,14},{10,... | collective-permute-start | bytes 786440 | tf_op jit(solution)/shard_map/ppermute | solution.py:289
  112.7 3.3 %collective-permute-start.17 = (bf16[2,512,128]{2,1,0:T(8,128)(2,1)S(1)}, bf16[2,512,128]{2,1,0:T(8,128)(2,1)S(1)}, u32[]{:S(2)}, u32[]{:S(2)}) collective-permute-start(bf16[2,512,128]{2,1,0:T(8,128)(2,1)S(1)} %get-tuple-element.64), channel_id=1, source_target_pairs={{0,5},{1,4},{2,7},{3,6},{4,1},{5,0},{6,3},{7,2},{8,13},{9,12},{10,... | collective-permute-start | bytes 786440 | tf_op jit(solution)/shard_map/ppermute | solution.py:289
  116.0 14.2 %flash_part.2 = (f32[8,512,256]{2,1,0:T(8,128)}, f32[8,512,128]{2,1,0:T(8,128)}) custom-call(s32[8]{0:T(128)} %add_convert_fusion.wanted_ref, f32[1,2048]{1,0:T(1,128)} %bitcast.53, bf16[4,128,1024]{2,1,0:T(8,128)(2,1)} %pad_maximum_fusion.q_ref, bf16[2,512,128]{2,1,0:T(8,128)(2,1)} %get-tuple-element.63.refs_0_, bf16[2,512,128]{2,1,0:T(8,128)(2,1)} %copy-done.12, ...), custom_call_target="tpu_custom_call" | custom-call | flops 8589934592 | bytes 1048576 | tf_op jit(solution)/shard_map/flash_part/pallas_call | solution.py:133
  130.9 2.5 %own_part.1 = (f32[2,64,1024]{2,1,0:T(8,128)}, f32[2,64,128]{2,1,0:T(8,128)}) custom-call(bf16[2,64,1024]{2,1,0:T(8,128)(2,1)} %q_ref, bf16[2,2,64,128]{3,2,1,0:T(8,128)(2,1)} %new_ref), custom_call_target="tpu_custom_call" | custom-call | tf_op jit(solution)/shard_map/own_part/pallas_call | solution.py:181
  133.4 13.6 %collective-permute-done.16.refs_0_ = bf16[2,512,128]{2,1,0:T(8,128)(2,1)S(1)} collective-permute-done((bf16[2,512,128]{2,1,0:T(8,128)(2,1)S(1)}, bf16[2,512,128]{2,1,0:T(8,128)(2,1)S(1)}, u32[]{:S(2)}, u32[]{:S(2)}) %collective-permute-start.16) | collective-permute-done | bytes 262176 | tf_op jit(solution)/shard_map/ppermute | solution.py:289
  147.0 24.4 %collective-permute-done.17.refs_1_ = bf16[2,512,128]{2,1,0:T(8,128)(2,1)S(1)} collective-permute-done((bf16[2,512,128]{2,1,0:T(8,128)(2,1)S(1)}, bf16[2,512,128]{2,1,0:T(8,128)(2,1)S(1)}, u32[]{:S(2)}, u32[]{:S(2)}) %collective-permute-start.17) | collective-permute-done | bytes 262176 | tf_op jit(solution)/shard_map/ppermute | solution.py:289
  172.2 14.2 %flash_part.3 = (f32[8,512,256]{2,1,0:T(8,128)}, f32[8,512,128]{2,1,0:T(8,128)}) custom-call(s32[8]{0:T(128)} %add_convert_fusion.wanted_ref, f32[1,1536]{1,0:T(1,128)} %broadcast_in_dim.79.bias_ref, bf16[4,128,1024]{2,1,0:T(8,128)(2,1)} %pad_maximum_fusion.q_ref, bf16[2,512,128]{2,1,0:T(8,128)(2,1)} %copy-done.8, bf16[2,512,128]{2,1,0:T(8,128)(2,1)} %copy-done.11, ...), custom_call_target="tpu_custom_call" | custom-call | flops 6442450944 | bytes 786432 | tf_op jit(solution)/shard_map/flash_part/pallas_call | solution.py:133
  187.1 7.5 %flash_last.3 = (bf16[128,1152]{1,0:T(8,128)(2,1)}, bf16[128,1152]{1,0:T(8,128)(2,1)}, bf16[128,1152]{1,0:T(8,128)(2,1)}) custom-call(s32[8]{0:T(128)} %add_convert_fusion.wanted_ref, f32[1,512]{1,0:T(1,128)} %bitcast.51, bf16[4,128,1024]{2,1,0:T(8,128)(2,1)} %pad_maximum_fusion.q_ref, bf16[2,512,128]{2,1,0:T(8,128)(2,1)} %copy-done.1, ...), custom_call_target="tpu_custom_call" | custom-call | flops 1610612736 | bytes 262144 | tf_op jit(solution)/shard_map/flash_last/pallas_call | solution.py:133
  199.9 12.2 %collective-permute-start.21 = (bf16[128,1152]{1,0:T(8,128)(2,1)}, bf16[128,1152]{1,0:T(8,128)(2,1)S(1)}, u32[]{:S(2)}, u32[]{:S(2)}) collective-permute-start(bf16[128,1152]{1,0:T(8,128)(2,1)} %get-tuple-element.53), channel_id=1, source_target_pairs={{0,24},{8,32},{16,40},{24,48},{32,56},{64,88},{72,96},{80,104},{88... | collective-permute-start | bytes 884744 | tf_op jit(solution)/shard_map/ppermute | solution.py:266
  214.5 4.9 %flash_last.2.m0 = bf16[128,1152]{1,0:T(8,128)(2,1)} custom-call(s32[8]{0:T(128)} %add_convert_fusion.wanted_ref, f32[1,512]{1,0:T(1,128)} %bitcast.52, bf16[4,128,1024]{2,1,0:T(8,128)(2,1)} %pad_maximum_fusion.q_ref, bf16[2,512,128]{2,1,0:T(8,128)(2,1)} %copy-done.1, f32[8,512,256]{2,1,0:T(8,128)} %get-tuple-element.49.refs_1_, ...), custom_call_target="tpu_custom_call" | custom-call | flops 536870912 | bytes 262144 | tf_op jit(solution)/shard_map/flash_last/pallas_call | solution.py:133
  219.5 14.7 %collective-permute-done.25.m4 = bf16[128,1152]{1,0:T(8,128)(2,1)S(1)} collective-permute-done((bf16[128,1152]{1,0:T(8,128)(2,1)S(1)}, bf16[128,1152]{1,0:T(8,128)(2,1)S(1)}, u32[]{:S(2)}, u32[]{:S(2)}) %collective-permute-start.25) | collective-permute-done | bytes 294944 | tf_op jit(solution)/shard_map/ppermute | solution.py:272
  234.9 3.3 %merge.1 = bf16[2,64,1024]{2,1,0:T(8,128)(2,1)} custom-call(s32[2]{0:T(128)} %get-tuple-element.44.code_ref, bf16[128,1152]{1,0:T(8,128)(2,1)} %flash_last.2.m0, bf16[128,1152]{1,0:T(8,128)(2,1)} %copy-done.2, bf16[128,1152]{1,0:T(8,128)(2,1)} %copy-done.3, bf16[128,1152]{1,0:T(8,128)(2,1)} %copy-done.4, bf16[128,1152]{1,0:T(8,128)(2,1)} %copy-done.5, ...), custom_call_target="tpu_custom_call" | custom-call | tf_op jit(solution)/shard_map/merge/pallas_call | solution.py:226
  (87 shorter events, 24.5 us)
Async XLA Ops:
  0.0 35.6 %collective-permute-start.10 = (s32[1,2]{1,0:T(1,128)}, s32[1,2]{1,0:T(1,128)S(1)}, u32[]{:S(2)}, u32[]{:S(2)}) collective-permute-start(s32[1,2]{1,0:T(1,128)} %param.9), channel_id=1, source_target_pairs={{24,0},{32,8},{40,16},{48,24},{56,32},{88,64},{96,72},{104,80},{11... | collective-permute-start | bytes 32 | tf_op jit(solution)/shard_map/ppermute | solution.py:266
  1.3 35.0 %collective-permute-start.9 = (s32[1,2]{1,0:T(1,128)}, s32[1,2]{1,0:T(1,128)S(1)}, u32[]{:S(2)}, u32[]{:S(2)}) collective-permute-start(s32[1,2]{1,0:T(1,128)} %param.9), channel_id=1, source_target_pairs={{16,0},{24,8},{32,16},{40,24},{48,32},{56,40},{80,64},{88,72},{96,... | collective-permute-start | bytes 32 | tf_op jit(solution)/shard_map/ppermute | solution.py:266
  2.6 35.7 %collective-permute-start.8 = (s32[1,2]{1,0:T(1,128)}, s32[1,2]{1,0:T(1,128)S(1)}, u32[]{:S(2)}, u32[]{:S(2)}) collective-permute-start(s32[1,2]{1,0:T(1,128)} %param.9), channel_id=1, source_target_pairs={{8,0},{16,8},{24,16},{32,24},{40,32},{48,40},{56,48},{72,64},{80,7... | collective-permute-start | bytes 32 | tf_op jit(solution)/shard_map/ppermute | solution.py:266
  5.2 125.0 %collective-permute-start.14 = (s32[1,2]{1,0:T(1,128)}, s32[1,2]{1,0:T(1,128)S(1)}, u32[]{:S(2)}, u32[]{:S(2)}) collective-permute-start(s32[1,2]{1,0:T(1,128)} %param.9), channel_id=1, source_target_pairs={{0,488},{8,496},{64,40},{72,48},{128,104},{136,112},{192,168},{200... | collective-permute-start | bytes 32 | tf_op jit(solution)/shard_map/ppermute | solution.py:272
  26.8 7.4 %collective-permute-start = (bf16[128,1024]{1,0:T(8,128)(2,1)}, bf16[128,1024]{1,0:T(8,128)(2,1)S(1)}, u32[]{:S(2)}, u32[]{:S(2)}) collective-permute-start(bf16[128,1024]{1,0:T(8,128)(2,1)} %bitcast.46), channel_id=1, source_target_pairs={{8,40},{72,104},{136,168},{200,232},{264,296},{328,360},{392,424},... | collective-permute-start | bytes 786440 | tf_op jit(solution)/shard_map/ppermute | solution.py:266
  34.2 34.1 %collective-permute-start.5 = (bf16[128,1024]{1,0:T(8,128)(2,1)S(1)}, bf16[128,1024]{1,0:T(8,128)(2,1)S(1)}, u32[]{:S(2)}, u32[]{:S(2)}) collective-permute-start(bf16[128,1024]{1,0:T(8,128)(2,1)S(1)} %bitcast.47), channel_id=1, source_target_pairs={{16,0},{24,8},{32,16},{40,24},{48,32},{56,40},{80,64},{88,72},{96,... | collective-permute-start | bytes 786440 | tf_op jit(solution)/shard_map/ppermute | solution.py:266
  36.3 9.2 %collective-permute-start.7 = (bf16[128,1024]{1,0:T(8,128)(2,1)S(1)}, bf16[128,1024]{1,0:T(8,128)(2,1)S(1)}, u32[]{:S(2)}, u32[]{:S(2)}) collective-permute-start(bf16[128,1024]{1,0:T(8,128)(2,1)S(1)} %bitcast.48), channel_id=1, source_target_pairs={{24,0},{32,8},{40,16},{48,24},{56,32},{88,64},{96,72},{104,80},{11... | collective-permute-start | bytes 786440 | tf_op jit(solution)/shard_map/ppermute | solution.py:266
  37.6 30.0 %collective-permute-start.6 = (bf16[128,1024]{1,0:T(8,128)(2,1)S(1)}, bf16[128,1024]{1,0:T(8,128)(2,1)S(1)}, u32[]{:S(2)}, u32[]{:S(2)}) collective-permute-start(bf16[128,1024]{1,0:T(8,128)(2,1)S(1)} %collective-permute-done.1), channel_id=1, source_target_pairs={{0,40},{40,48},{16,56},{64,104},{104,112},{80,120},{128,168},{168,... | collective-permute-start | bytes 786440 | tf_op jit(solution)/shard_map/ppermute | solution.py:266
  38.3 32.0 %collective-permute-start.4 = (bf16[128,1024]{1,0:T(8,128)(2,1)S(1)}, bf16[128,1024]{1,0:T(8,128)(2,1)S(1)}, u32[]{:S(2)}, u32[]{:S(2)}) collective-permute-start(bf16[128,1024]{1,0:T(8,128)(2,1)S(1)} %collective-permute-done.1), channel_id=1, source_target_pairs={{0,48},{40,56},{64,112},{104,120},{128,176},{168,184},{192,240},{2... | collective-permute-start | bytes 786440 | tf_op jit(solution)/shard_map/ppermute | solution.py:266
  45.5 26.8 %collective-permute-start.3 = (bf16[128,1024]{1,0:T(8,128)(2,1)S(1)}, bf16[128,1024]{1,0:T(8,128)(2,1)S(1)}, u32[]{:S(2)}, u32[]{:S(2)}) collective-permute-start(bf16[128,1024]{1,0:T(8,128)(2,1)S(1)} %bitcast.49), channel_id=1, source_target_pairs={{8,0},{16,8},{24,16},{32,24},{40,32},{48,40},{56,48},{72,64},{80,7... | collective-permute-start | bytes 786440 | tf_op jit(solution)/shard_map/ppermute | solution.py:266
  67.6 12.4 %collective-permute-start.2 = (bf16[128,1024]{1,0:T(8,128)(2,1)S(1)}, bf16[128,1024]{1,0:T(8,128)(2,1)S(1)}, u32[]{:S(2)}, u32[]{:S(2)}) collective-permute-start(bf16[128,1024]{1,0:T(8,128)(2,1)S(1)} %collective-permute-done.1), channel_id=1, source_target_pairs={{0,56},{64,120},{128,184},{192,248},{256,312},{320,376},{384,440},... | collective-permute-start | bytes 786440 | tf_op jit(solution)/shard_map/ppermute | solution.py:266
  68.4 65.0 %collective-permute-start.18 = (bf16[2,512,128]{2,1,0:T(8,128)(2,1)S(1)}, bf16[2,512,128]{2,1,0:T(8,128)(2,1)S(1)}, u32[]{:S(2)}, u32[]{:S(2)}) collective-permute-start(bf16[2,512,128]{2,1,0:T(8,128)(2,1)S(1)} %get-tuple-element.57), channel_id=1, source_target_pairs={{0,6},{1,7},{2,4},{3,5},{4,2},{5,3},{6,0},{7,1},{8,14},{9,15},{10,... | collective-permute-start | bytes 786440 | tf_op jit(solution)/shard_map/ppermute | solution.py:289
  70.3 25.1 %collective-permute-start.13 = (bf16[2,512,128]{2,1,0:T(8,128)(2,1)S(1)}, bf16[2,512,128]{2,1,0:T(8,128)(2,1)S(1)}, u32[]{:S(2)}, u32[]{:S(2)}) collective-permute-start(bf16[2,512,128]{2,1,0:T(8,128)(2,1)S(1)} %get-tuple-element.60), channel_id=1, source_target_pairs={{0,3},{1,2},{2,1},{3,0},{4,7},{5,6},{6,5},{7,4},{8,11},{9,10},{10,... | collective-permute-start | bytes 786440 | tf_op jit(solution)/shard_map/ppermute | solution.py:289
  72.3 34.2 %collective-permute-start.12 = (bf16[2,512,128]{2,1,0:T(8,128)(2,1)S(1)}, bf16[2,512,128]{2,1,0:T(8,128)(2,1)S(1)}, u32[]{:S(2)}, u32[]{:S(2)}) collective-permute-start(bf16[2,512,128]{2,1,0:T(8,128)(2,1)S(1)} %get-tuple-element.61), channel_id=1, source_target_pairs={{0,2},{1,3},{2,0},{3,1},{4,6},{5,7},{6,4},{7,5},{8,10},{9,11},{10,... | collective-permute-start | bytes 786440 | tf_op jit(solution)/shard_map/ppermute | solution.py:289
  80.0 32.6 %collective-permute-start.11 = (bf16[2,512,128]{2,1,0:T(8,128)(2,1)S(1)}, bf16[2,512,128]{2,1,0:T(8,128)(2,1)S(1)}, u32[]{:S(2)}, u32[]{:S(2)}) collective-permute-start(bf16[2,512,128]{2,1,0:T(8,128)(2,1)S(1)} %get-tuple-element.62), channel_id=1, source_target_pairs={{0,1},{1,0},{2,3},{3,2},{4,5},{5,4},{6,7},{7,6},{8,9},{9,8},{10,11... | collective-permute-start | bytes 786440 | tf_op jit(solution)/shard_map/ppermute | solution.py:289
  95.4 51.7 %collective-permute-start.16 = (bf16[2,512,128]{2,1,0:T(8,128)(2,1)S(1)}, bf16[2,512,128]{2,1,0:T(8,128)(2,1)S(1)}, u32[]{:S(2)}, u32[]{:S(2)}) collective-permute-start(bf16[2,512,128]{2,1,0:T(8,128)(2,1)S(1)} %get-tuple-element.58), channel_id=1, source_target_pairs={{0,4},{1,5},{2,6},{3,7},{4,0},{5,1},{6,2},{7,3},{8,12},{9,13},{10,... | collective-permute-start | bytes 786440 | tf_op jit(solution)/shard_map/ppermute | solution.py:289
  106.5 79.9 %collective-permute-start.15 = (bf16[2,512,128]{2,1,0:T(8,128)(2,1)S(1)}, bf16[2,512,128]{2,1,0:T(8,128)(2,1)S(1)}, u32[]{:S(2)}, u32[]{:S(2)}) collective-permute-start(bf16[2,512,128]{2,1,0:T(8,128)(2,1)S(1)} %get-tuple-element.59), channel_id=1, source_target_pairs={{0,7},{1,6},{2,5},{3,4},{4,3},{5,2},{6,1},{7,0},{8,15},{9,14},{10,... | collective-permute-start | bytes 786440 | tf_op jit(solution)/shard_map/ppermute | solution.py:289
  112.7 58.8 %collective-permute-start.17 = (bf16[2,512,128]{2,1,0:T(8,128)(2,1)S(1)}, bf16[2,512,128]{2,1,0:T(8,128)(2,1)S(1)}, u32[]{:S(2)}, u32[]{:S(2)}) collective-permute-start(bf16[2,512,128]{2,1,0:T(8,128)(2,1)S(1)} %get-tuple-element.64), channel_id=1, source_target_pairs={{0,5},{1,4},{2,7},{3,6},{4,1},{5,0},{6,3},{7,2},{8,13},{9,12},{10,... | collective-permute-start | bytes 786440 | tf_op jit(solution)/shard_map/ppermute | solution.py:289
  195.2 16.9 %collective-permute-start.23 = (bf16[128,1152]{1,0:T(8,128)(2,1)}, bf16[128,1152]{1,0:T(8,128)(2,1)S(1)}, u32[]{:S(2)}, u32[]{:S(2)}) collective-permute-start(bf16[128,1152]{1,0:T(8,128)(2,1)} %get-tuple-element.52), channel_id=1, source_target_pairs={{48,40},{56,48},{112,104},{120,112},{176,168},{184,176},{240,232},... | collective-permute-start | bytes 884744 | tf_op jit(solution)/shard_map/ppermute | solution.py:266
  195.9 16.2 %collective-permute-start.24 = (bf16[128,1152]{1,0:T(8,128)(2,1)}, bf16[128,1152]{1,0:T(8,128)(2,1)S(1)}, u32[]{:S(2)}, u32[]{:S(2)}) collective-permute-start(bf16[128,1152]{1,0:T(8,128)(2,1)} %get-tuple-element.53), channel_id=1, source_target_pairs={{56,16},{120,80},{184,144},{248,208},{312,272},{376,336},{440,400}... | collective-permute-start | bytes 884744 | tf_op jit(solution)/shard_map/ppermute | solution.py:266
  196.6 22.9 %collective-permute-start.19 = (bf16[128,1152]{1,0:T(8,128)(2,1)}, bf16[128,1152]{1,0:T(8,128)(2,1)S(1)}, u32[]{:S(2)}, u32[]{:S(2)}) collective-permute-start(bf16[128,1152]{1,0:T(8,128)(2,1)} %get-tuple-element.51), channel_id=1, source_target_pairs={{0,8},{8,16},{16,24},{24,32},{32,40},{40,48},{48,56},{64,72},{72,8... | collective-permute-start | bytes 884744 | tf_op jit(solution)/shard_map/ppermute | solution.py:266
  198.5 20.9 %collective-permute-start.20 = (bf16[128,1152]{1,0:T(8,128)(2,1)}, bf16[128,1152]{1,0:T(8,128)(2,1)S(1)}, u32[]{:S(2)}, u32[]{:S(2)}) collective-permute-start(bf16[128,1152]{1,0:T(8,128)(2,1)} %get-tuple-element.52), channel_id=1, source_target_pairs={{0,16},{8,24},{16,32},{24,40},{32,48},{40,56},{64,80},{72,88},{80,... | collective-permute-start | bytes 884744 | tf_op jit(solution)/shard_map/ppermute | solution.py:266
  199.9 19.6 %collective-permute-start.21 = (bf16[128,1152]{1,0:T(8,128)(2,1)}, bf16[128,1152]{1,0:T(8,128)(2,1)S(1)}, u32[]{:S(2)}, u32[]{:S(2)}) collective-permute-start(bf16[128,1152]{1,0:T(8,128)(2,1)} %get-tuple-element.53), channel_id=1, source_target_pairs={{0,24},{8,32},{16,40},{24,48},{32,56},{64,88},{72,96},{80,104},{88... | collective-permute-start | bytes 884744 | tf_op jit(solution)/shard_map/ppermute | solution.py:266
  213.2 21.0 %collective-permute-start.25 = (bf16[128,1152]{1,0:T(8,128)(2,1)S(1)}, bf16[128,1152]{1,0:T(8,128)(2,1)S(1)}, u32[]{:S(2)}, u32[]{:S(2)}) collective-permute-start(bf16[128,1152]{1,0:T(8,128)(2,1)S(1)} %select_select_fusion), channel_id=1, source_target_pairs={{40,64},{48,72},{16,80},{104,128},{112,136},{80,144},{168,192},{17... | collective-permute-start | bytes 884744 | tf_op jit(solution)/shard_map/ppermute | solution.py:272
  (15 other events, 157.0 us)

commit v2 on v1

--- a/solution.py
+++ b/solution.py
@@ -18,7 +18,7 @@
 QROWS = 64
 MSG = HEADS * HD + 128
 MASKED = -1e30
-ORDER = ((0, 1, 2, 3), (4, 5, 6), (7,))
+ORDER = ((0, 1, 2, 3, 4), (5, 6), (7,))
 SCALE2 = 1.4426950408889634 * HD ** (-0.5)
 
 
@@ -278,7 +278,6 @@
     over = cross_row(jnp.where(place == 5, hop, flat_q), [(0, 0), (5, 5), (2, 2)], -1)
     inside = [[(i, i - k) for i in range(k, ROW)] for k in range(1, REACH)]
     tags = [in_row(offsets, inside[k - 1]) for k in range(1, REACH)]
-    far_offsets = cross_row(offsets, [(0, 5), (1, 6)], -1)
     near = [in_row(flat_q, [(i, i - k) for i in range(k, ROW)]) for k in range(1, REACH)]
 
     def slab(j):
@@ -292,6 +291,7 @@
     chunk[0] = slab(0)
     far = [in_row(over, [((0, 5, 2)[i], ROW - k + i) for i in range(k)]) for k in range(1, REACH)]
 
+    tags, far = lax.optimization_barrier((tags, far))
     live = live_bias(block_table[0], lengths[0], member, members)
     biases = [jnp.concatenate([live[j] for j in order])[None, :] for order in ORDER]
     slots = REACH * caps
@@ -303,14 +303,16 @@
     q_all, wanted, biases = lax.optimization_barrier((q_all, wanted, biases))
 
     state = flash_call(wanted, biases[0], q_all, [chunk[j] for j in ORDER[0]], None, (0, slots), caps)
-    state, later = lax.optimization_barrier((state, (queries, new_cache, far_offsets, offsets)))
-    own = own_call(*later[:2])
-    asked = later[2][0]
-    code = jnp.where(place == 2, 3, jnp.where(asked == 3, 0, asked))
+    state, mine, told = lax.optimization_barrier((state, (queries, new_cache), offsets))
+    far_offsets = cross_row(told, [(0, 5), (1, 6)], -1)
+    own = own_call(*mine)
+    state, own = lax.optimization_barrier((state, own))
+    state = flash_call(wanted, biases[1], q_all, [chunk[j] for j in ORDER[1]], state, (0, slots), caps)
+    state, own_offsets, far_offsets = lax.optimization_barrier((state, offsets[0], far_offsets[0]))
+    code = jnp.where(place == 2, 3, jnp.where(far_offsets == 3, 0, far_offsets))
     pick = jnp.broadcast_to(jnp.repeat(code, QROWS)[:, None], (last_row, HD))
-    source = jnp.where(later[3][0] <= place, later[3][0], REACH)
-    state, own, pick, source = lax.optimization_barrier((state, own, pick, source))
-    state = flash_call(wanted, biases[1], q_all, [chunk[j] for j in ORDER[1]], state, (0, slots), caps)
+    source = jnp.where(own_offsets <= place, own_offsets, REACH)
+    state, pick, source = lax.optimization_barrier((state, pick, source))
     final = partial(flash_call, wanted, biases[2], q_all, [chunk[j] for j in ORDER[2]], state)
     message = [None, *final((caps, slots - caps), caps, True)]
 

time: 239 us -> 255 us (1.067)
  the two profiles are of different devices: /device:TPU:33 before, /device:TPU:1 now
where the time goes in v2:
time: 255 us; the launch traced here: 254 us
  starting transfers between devices  133 us (52%)
  waiting for transfers between devices  58.9 us (23%)
  Pallas kernels  46.5 us (18%)
  local copies, waits for them, and re-layouts  8.08 us (3%)
  other arithmetic  6.04 us (2%)
    ppermute x3, starting transfers between devices, cross_row(): return lax.ppermute(value, 'group', whole)  77.3 us
    pallas_call x4, Pallas kernels, flash_call(): pl.pallas_call(partial(flash_kernel, n, lo, first, caps if last else None...  40.8 us
    ppermute x16, waiting for transfers between devices, in_row(): return lax.ppermute(value, 'group', whole)  38.5 us
    ppermute x7, starting transfers between devices, exchanged(): return lax.ppermute(value, 'tensor', [(m, m ^ j) for m in range(members)])  28.6 us
    ppermute x16, starting transfers between devices, in_row(): return lax.ppermute(value, 'group', whole)  27 us
    ppermute x3, waiting for transfers between devices, cross_row(): return lax.ppermute(value, 'group', whole)  12.7 us
    ppermute x7, waiting for transfers between devices, exchanged(): return lax.ppermute(value, 'tensor', [(m, m ^ j) for m in range(members)])  7.68 us
  transfers between devices with their start and end apart: 26, of which 6 were waited for; matrix products, arithmetic and copies ran while one was open for 4% of the time, Pallas kernels for 14%

profile of v2, /device:TPU:1, one launch (start us, length us, event | category | flops | bytes accessed | tf_op | source)
XLA Modules:
  0.0 253.7 jit_solution(10883188301685862680)
XLA Ops:
  0.0 5.5 %collective-permute-start.3 = (bf16[128,1024]{1,0:T(8,128)(2,1)}, bf16[128,1024]{1,0:T(8,128)(2,1)S(1)}, u32[]{:S(2)}, u32[]{:S(2)}) collective-permute-start(bf16[128,1024]{1,0:T(8,128)(2,1)} %bitcast.53), channel_id=1, source_target_pairs={{8,40},{72,104},{136,168},{200,232},{264,296},{328,360},{392,424},... | collective-permute-start | bytes 786440 | tf_op jit(solution)/shard_map/ppermute | solution.py:266
  6.8 3.9 %collective-permute-start = (s32[1,2]{1,0:T(1,128)}, s32[1,2]{1,0:T(1,128)S(1)}, u32[]{:S(2)}, u32[]{:S(2)}) collective-permute-start(s32[1,2]{1,0:T(1,128)} %param.9), channel_id=1, source_target_pairs={{8,0},{16,8},{24,16},{32,24},{40,32},{48,40},{56,48},{72,64},{80,7... | collective-permute-start | bytes 32 | tf_op jit(solution)/shard_map/ppermute | solution.py:266
  14.9 2.4 constant_dynamic-slice_fusion.7
  21.9 4.2 %collective-permute-done.1 = s32[1,2]{1,0:T(1,128)S(1)} collective-permute-done((s32[1,2]{1,0:T(1,128)S(1)}, s32[1,2]{1,0:T(1,128)S(1)}, u32[]{:S(2)}, u32[]{:S(2)}) %collective-permute-start.1) | collective-permute-done | bytes 40 | tf_op jit(solution)/shard_map/ppermute | solution.py:266
  27.4 27.7 %collective-permute-done.2 = s32[1,2]{1,0:T(1,128)S(1)} collective-permute-done((s32[1,2]{1,0:T(1,128)S(1)}, s32[1,2]{1,0:T(1,128)S(1)}, u32[]{:S(2)}, u32[]{:S(2)}) %collective-permute-start.2) | collective-permute-done | bytes 40 | tf_op jit(solution)/shard_map/ppermute | solution.py:266
  55.2 3.9 %collective-permute-start.8 = (bf16[128,1024]{1,0:T(8,128)(2,1)S(1)}, bf16[128,1024]{1,0:T(8,128)(2,1)S(1)}, u32[]{:S(2)}, u32[]{:S(2)}) collective-permute-start(bf16[128,1024]{1,0:T(8,128)(2,1)S(1)} %bitcast.55), channel_id=1, source_target_pairs={{8,0},{16,8},{24,16},{32,24},{40,32},{48,40},{56,48},{72,64},{80,7... | collective-permute-start | bytes 786440 | tf_op jit(solution)/shard_map/ppermute | solution.py:266
  60.4 2.6 %collective-permute-start.13 = (bf16[2,512,128]{2,1,0:T(8,128)(2,1)S(1)}, bf16[2,512,128]{2,1,0:T(8,128)(2,1)S(1)}, u32[]{:S(2)}, u32[]{:S(2)}) collective-permute-start(bf16[2,512,128]{2,1,0:T(8,128)(2,1)S(1)} %get-tuple-element.82), channel_id=1, source_target_pairs={{0,1},{1,0},{2,3},{3,2},{4,5},{5,4},{6,7},{7,6},{8,9},{9,8},{10,11... | collective-permute-start | bytes 786440 | tf_op jit(solution)/shard_map/ppermute | solution.py:288
  63.0 4.0 %collective-permute-start.14 = (bf16[2,512,128]{2,1,0:T(8,128)(2,1)S(1)}, bf16[2,512,128]{2,1,0:T(8,128)(2,1)S(1)}, u32[]{:S(2)}, u32[]{:S(2)}) collective-permute-start(bf16[2,512,128]{2,1,0:T(8,128)(2,1)S(1)} %get-tuple-element.81), channel_id=1, source_target_pairs={{0,2},{1,3},{2,0},{3,1},{4,6},{5,7},{6,4},{7,5},{8,10},{9,11},{10,... | collective-permute-start | bytes 786440 | tf_op jit(solution)/shard_map/ppermute | solution.py:288
  67.0 2.7 %collective-permute-start.15 = (bf16[2,512,128]{2,1,0:T(8,128)(2,1)S(1)}, bf16[2,512,128]{2,1,0:T(8,128)(2,1)S(1)}, u32[]{:S(2)}, u32[]{:S(2)}) collective-permute-start(bf16[2,512,128]{2,1,0:T(8,128)(2,1)S(1)} %get-tuple-element.80), channel_id=1, source_target_pairs={{0,3},{1,2},{2,1},{3,0},{4,7},{5,6},{6,5},{7,4},{8,11},{9,10},{10,... | collective-permute-start | bytes 786440 | tf_op jit(solution)/shard_map/ppermute | solution.py:288
  69.8 5.3 %collective-permute-start.16 = (bf16[2,512,128]{2,1,0:T(8,128)(2,1)S(1)}, bf16[2,512,128]{2,1,0:T(8,128)(2,1)S(1)}, u32[]{:S(2)}, u32[]{:S(2)}) collective-permute-start(bf16[2,512,128]{2,1,0:T(8,128)(2,1)S(1)} %get-tuple-element.86), channel_id=1, source_target_pairs={{0,4},{1,5},{2,6},{3,7},{4,0},{5,1},{6,2},{7,3},{8,12},{9,13},{10,... | collective-permute-start | bytes 786440 | tf_op jit(solution)/shard_map/ppermute | solution.py:288
  75.1 3.4 %collective-permute-start.11 = (bf16[2,512,128]{2,1,0:T(8,128)(2,1)S(1)}, bf16[2,512,128]{2,1,0:T(8,128)(2,1)S(1)}, u32[]{:S(2)}, u32[]{:S(2)}) collective-permute-start(bf16[2,512,128]{2,1,0:T(8,128)(2,1)S(1)} %get-tuple-element.85), channel_id=1, source_target_pairs={{0,5},{1,4},{2,7},{3,6},{4,1},{5,0},{6,3},{7,2},{8,13},{9,12},{10,... | collective-permute-start | bytes 786440 | tf_op jit(solution)/shard_map/ppermute | solution.py:288
  80.2 6.7 %collective-permute-start.12 = (bf16[2,512,128]{2,1,0:T(8,128)(2,1)S(1)}, bf16[2,512,128]{2,1,0:T(8,128)(2,1)S(1)}, u32[]{:S(2)}, u32[]{:S(2)}) collective-permute-start(bf16[2,512,128]{2,1,0:T(8,128)(2,1)S(1)} %get-tuple-element.84), channel_id=1, source_target_pairs={{0,6},{1,7},{2,4},{3,5},{4,2},{5,3},{6,0},{7,1},{8,14},{9,15},{10,... | collective-permute-start | bytes 786440 | tf_op jit(solution)/shard_map/ppermute | solution.py:288
  86.9 7.7 %collective-permute-done.14.refs_2_ = bf16[2,512,128]{2,1,0:T(8,128)(2,1)S(1)} collective-permute-done((bf16[2,512,128]{2,1,0:T(8,128)(2,1)S(1)}, bf16[2,512,128]{2,1,0:T(8,128)(2,1)S(1)}, u32[]{:S(2)}, u32[]{:S(2)}) %collective-permute-start.14) | collective-permute-done | bytes 262176 | tf_op jit(solution)/shard_map/ppermute | solution.py:288
  94.6 4.0 %collective-permute-start.18 = (bf16[2,512,128]{2,1,0:T(8,128)(2,1)S(1)}, bf16[2,512,128]{2,1,0:T(8,128)(2,1)S(1)}, u32[]{:S(2)}, u32[]{:S(2)}) collective-permute-start(bf16[2,512,128]{2,1,0:T(8,128)(2,1)S(1)} %get-tuple-element.79), channel_id=1, source_target_pairs={{0,7},{1,6},{2,5},{3,4},{4,3},{5,2},{6,1},{7,0},{8,15},{9,14},{10,... | collective-permute-start | bytes 786440 | tf_op jit(solution)/shard_map/ppermute | solution.py:288
  100.0 16.1 %flash_part.2 = (f32[8,512,256]{2,1,0:T(8,128)}, f32[8,512,128]{2,1,0:T(8,128)}) custom-call(s32[8]{0:T(128)} %add_convert_fusion.wanted_ref, f32[1,2560]{1,0:T(1,128)} %broadcast_in_dim.78.bias_ref, bf16[4,128,1024]{2,1,0:T(8,128)(2,1)} %pad_maximum_fusion.q_ref, bf16[2,512,128]{2,1,0:T(8,128)(2,1)} %get-tuple-element.83.refs_0_, ...), custom_call_target="tpu_custom_call" | custom-call | flops 10737418240 | bytes 1310720 | tf_op jit(solution)/shard_map/flash_part/pallas_call | solution.py:133
  116.1 2.5 own_part.1
  118.5 75.2 %collective-permute-start.17 = (s32[1,2]{1,0:T(1,128)S(1)}, s32[1,2]{1,0:T(1,128)S(1)}, u32[]{:S(2)}, u32[]{:S(2)}) collective-permute-start(s32[1,2]{1,0:T(1,128)S(1)} %copy-done.12), channel_id=1, source_target_pairs={{0,488},{8,496},{64,40},{72,48},{128,104},{136,112},{192,168},{200... | collective-permute-start | bytes 32 | tf_op jit(solution)/shard_map/ppermute | solution.py:272
  195.2 12.3 %flash_part.3 = (f32[8,512,256]{2,1,0:T(8,128)}, f32[8,512,128]{2,1,0:T(8,128)}) custom-call(s32[8]{0:T(128)} %add_convert_fusion.wanted_ref, f32[1,1024]{1,0:T(1,128)} %bitcast.60, bf16[4,128,1024]{2,1,0:T(8,128)(2,1)} %pad_maximum_fusion.q_ref, bf16[2,512,128]{2,1,0:T(8,128)(2,1)} %copy-done.9, bf16[2,512,128]{2,1,0:T(8,128)(2,1)} %copy-done.11, ...), custom_call_target="tpu_custom_call" | custom-call | flops 4294967296 | bytes 524288 | tf_op jit(solution)/shard_map/flash_part/pallas_call | solution.py:133
  209.0 7.5 %flash_last.3 = (bf16[128,1152]{1,0:T(8,128)(2,1)}, bf16[128,1152]{1,0:T(8,128)(2,1)}, bf16[128,1152]{1,0:T(8,128)(2,1)}) custom-call(s32[8]{0:T(128)} %add_convert_fusion.wanted_ref, f32[1,512]{1,0:T(1,128)} %bitcast.58, bf16[4,128,1024]{2,1,0:T(8,128)(2,1)} %pad_maximum_fusion.q_ref, bf16[2,512,128]{2,1,0:T(8,128)(2,1)} %copy-done.1, ...), custom_call_target="tpu_custom_call" | custom-call | flops 1610612736 | bytes 262144 | tf_op jit(solution)/shard_map/flash_last/pallas_call | solution.py:133
  218.5 1.9 collective-permute-start.19
  225.5 4.9 %flash_last.2.m0 = bf16[128,1152]{1,0:T(8,128)(2,1)} custom-call(s32[8]{0:T(128)} %add_convert_fusion.wanted_ref, f32[1,512]{1,0:T(1,128)} %bitcast.59, bf16[4,128,1024]{2,1,0:T(8,128)(2,1)} %pad_maximum_fusion.q_ref, bf16[2,512,128]{2,1,0:T(8,128)(2,1)} %copy-done.1, f32[8,512,256]{2,1,0:T(8,128)} %get-tuple-element.71.refs_1_, ...), custom_call_target="tpu_custom_call" | custom-call | flops 536870912 | bytes 262144 | tf_op jit(solution)/shard_map/flash_last/pallas_call | solution.py:133
  231.9 5.2 %collective-permute-done.21.m3 = bf16[128,1152]{1,0:T(8,128)(2,1)S(1)} collective-permute-done((bf16[128,1152]{1,0:T(8,128)(2,1)}, bf16[128,1152]{1,0:T(8,128)(2,1)S(1)}, u32[]{:S(2)}, u32[]{:S(2)}) %collective-permute-start.21) | collective-permute-done | bytes 294944 | tf_op jit(solution)/shard_map/ppermute | solution.py:266
  237.0 12.7 %collective-permute-done.25.m4 = bf16[128,1152]{1,0:T(8,128)(2,1)S(1)} collective-permute-done((bf16[128,1152]{1,0:T(8,128)(2,1)S(1)}, bf16[128,1152]{1,0:T(8,128)(2,1)S(1)}, u32[]{:S(2)}, u32[]{:S(2)}) %collective-permute-start.25) | collective-permute-done | bytes 294944 | tf_op jit(solution)/shard_map/ppermute | solution.py:272
  250.4 3.3 %merge.1 = bf16[2,64,1024]{2,1,0:T(8,128)(2,1)} custom-call(s32[2]{0:T(128)} %compare_select_fusion.code_ref, bf16[128,1152]{1,0:T(8,128)(2,1)} %flash_last.2.m0, bf16[128,1152]{1,0:T(8,128)(2,1)} %copy-done.2, bf16[128,1152]{1,0:T(8,128)(2,1)} %copy-done.3, bf16[128,1152]{1,0:T(8,128)(2,1)} %copy-done.4, bf16[128,1152]{1,0:T(8,128)(2,1)} %copy-done.5, ...), custom_call_target="tpu_custom_call" | custom-call | tf_op jit(solution)/shard_map/merge/pallas_call | solution.py:226
  (92 shorter events, 27.1 us)
Async XLA Ops:
  0.0 13.1 %collective-permute-start.3 = (bf16[128,1024]{1,0:T(8,128)(2,1)}, bf16[128,1024]{1,0:T(8,128)(2,1)S(1)}, u32[]{:S(2)}, u32[]{:S(2)}) collective-permute-start(bf16[128,1024]{1,0:T(8,128)(2,1)} %bitcast.53), channel_id=1, source_target_pairs={{8,40},{72,104},{136,168},{200,232},{264,296},{328,360},{392,424},... | collective-permute-start | bytes 786440 | tf_op jit(solution)/shard_map/ppermute | solution.py:266
  5.5 61.5 %collective-permute-start.9 = (bf16[128,1024]{1,0:T(8,128)(2,1)}, bf16[128,1024]{1,0:T(8,128)(2,1)S(1)}, u32[]{:S(2)}, u32[]{:S(2)}) collective-permute-start(bf16[128,1024]{1,0:T(8,128)(2,1)} %bitcast.54), channel_id=1, source_target_pairs={{16,0},{24,8},{32,16},{40,24},{48,32},{56,40},{80,64},{88,72},{96,... | collective-permute-start | bytes 786440 | tf_op jit(solution)/shard_map/ppermute | solution.py:266
  6.8 13.9 %collective-permute-start = (s32[1,2]{1,0:T(1,128)}, s32[1,2]{1,0:T(1,128)S(1)}, u32[]{:S(2)}, u32[]{:S(2)}) collective-permute-start(s32[1,2]{1,0:T(1,128)} %param.9), channel_id=1, source_target_pairs={{8,0},{16,8},{24,16},{32,24},{40,32},{48,40},{56,48},{72,64},{80,7... | collective-permute-start | bytes 32 | tf_op jit(solution)/shard_map/ppermute | solution.py:266
  17.4 41.7 %collective-permute-start.5 = (bf16[128,1024]{1,0:T(8,128)(2,1)S(1)}, bf16[128,1024]{1,0:T(8,128)(2,1)S(1)}, u32[]{:S(2)}, u32[]{:S(2)}) collective-permute-start(bf16[128,1024]{1,0:T(8,128)(2,1)S(1)} %collective-permute-done.4), channel_id=1, source_target_pairs={{0,56},{64,120},{128,184},{192,248},{256,312},{320,376},{384,440},... | collective-permute-start | bytes 786440 | tf_op jit(solution)/shard_map/ppermute | solution.py:266
  18.1 42.3 %collective-permute-start.6 = (bf16[128,1024]{1,0:T(8,128)(2,1)S(1)}, bf16[128,1024]{1,0:T(8,128)(2,1)S(1)}, u32[]{:S(2)}, u32[]{:S(2)}) collective-permute-start(bf16[128,1024]{1,0:T(8,128)(2,1)S(1)} %collective-permute-done.4), channel_id=1, source_target_pairs={{0,48},{40,56},{64,112},{104,120},{128,176},{168,184},{192,240},{2... | collective-permute-start | bytes 786440 | tf_op jit(solution)/shard_map/ppermute | solution.py:266
  18.8 44.2 %collective-permute-start.7 = (bf16[128,1024]{1,0:T(8,128)(2,1)S(1)}, bf16[128,1024]{1,0:T(8,128)(2,1)S(1)}, u32[]{:S(2)}, u32[]{:S(2)}) collective-permute-start(bf16[128,1024]{1,0:T(8,128)(2,1)S(1)} %collective-permute-done.4), channel_id=1, source_target_pairs={{0,40},{40,48},{16,56},{64,104},{104,112},{80,120},{128,168},{168,... | collective-permute-start | bytes 786440 | tf_op jit(solution)/shard_map/ppermute | solution.py:266
  20.6 5.5 %collective-permute-start.1 = (s32[1,2]{1,0:T(1,128)S(1)}, s32[1,2]{1,0:T(1,128)S(1)}, u32[]{:S(2)}, u32[]{:S(2)}) collective-permute-start(s32[1,2]{1,0:T(1,128)S(1)} %copy-done.12), channel_id=1, source_target_pairs={{16,0},{24,8},{32,16},{40,24},{48,32},{56,40},{80,64},{88,72},{96,... | collective-permute-start | bytes 32 | tf_op jit(solution)/shard_map/ppermute | solution.py:266
  26.2 29.0 %collective-permute-start.2 = (s32[1,2]{1,0:T(1,128)S(1)}, s32[1,2]{1,0:T(1,128)S(1)}, u32[]{:S(2)}, u32[]{:S(2)}) collective-permute-start(s32[1,2]{1,0:T(1,128)S(1)} %copy-done.12), channel_id=1, source_target_pairs={{24,0},{32,8},{40,16},{48,24},{56,32},{88,64},{96,72},{104,80},{11... | collective-permute-start | bytes 32 | tf_op jit(solution)/shard_map/ppermute | solution.py:266
  55.2 19.9 %collective-permute-start.8 = (bf16[128,1024]{1,0:T(8,128)(2,1)S(1)}, bf16[128,1024]{1,0:T(8,128)(2,1)S(1)}, u32[]{:S(2)}, u32[]{:S(2)}) collective-permute-start(bf16[128,1024]{1,0:T(8,128)(2,1)S(1)} %bitcast.55), channel_id=1, source_target_pairs={{8,0},{16,8},{24,16},{32,24},{40,32},{48,40},{56,48},{72,64},{80,7... | collective-permute-start | bytes 786440 | tf_op jit(solution)/shard_map/ppermute | solution.py:266
  59.1 10.7 %collective-permute-start.10 = (bf16[128,1024]{1,0:T(8,128)(2,1)S(1)}, bf16[128,1024]{1,0:T(8,128)(2,1)S(1)}, u32[]{:S(2)}, u32[]{:S(2)}) collective-permute-start(bf16[128,1024]{1,0:T(8,128)(2,1)S(1)} %bitcast.56), channel_id=1, source_target_pairs={{24,0},{32,8},{40,16},{48,24},{56,32},{88,64},{96,72},{104,80},{11... | collective-permute-start | bytes 786440 | tf_op jit(solution)/shard_map/ppermute | solution.py:266
  60.4 19.9 %collective-permute-start.13 = (bf16[2,512,128]{2,1,0:T(8,128)(2,1)S(1)}, bf16[2,512,128]{2,1,0:T(8,128)(2,1)S(1)}, u32[]{:S(2)}, u32[]{:S(2)}) collective-permute-start(bf16[2,512,128]{2,1,0:T(8,128)(2,1)S(1)} %get-tuple-element.82), channel_id=1, source_target_pairs={{0,1},{1,0},{2,3},{3,2},{4,5},{5,4},{6,7},{7,6},{8,9},{9,8},{10,11... | collective-permute-start | bytes 786440 | tf_op jit(solution)/shard_map/ppermute | solution.py:288
  63.0 31.6 %collective-permute-start.14 = (bf16[2,512,128]{2,1,0:T(8,128)(2,1)S(1)}, bf16[2,512,128]{2,1,0:T(8,128)(2,1)S(1)}, u32[]{:S(2)}, u32[]{:S(2)}) collective-permute-start(bf16[2,512,128]{2,1,0:T(8,128)(2,1)S(1)} %get-tuple-element.81), channel_id=1, source_target_pairs={{0,2},{1,3},{2,0},{3,1},{4,6},{5,7},{6,4},{7,5},{8,10},{9,11},{10,... | collective-permute-start | bytes 786440 | tf_op jit(solution)/shard_map/ppermute | solution.py:288
  67.0 31.5 %collective-permute-start.15 = (bf16[2,512,128]{2,1,0:T(8,128)(2,1)S(1)}, bf16[2,512,128]{2,1,0:T(8,128)(2,1)S(1)}, u32[]{:S(2)}, u32[]{:S(2)}) collective-permute-start(bf16[2,512,128]{2,1,0:T(8,128)(2,1)S(1)} %get-tuple-element.80), channel_id=1, source_target_pairs={{0,3},{1,2},{2,1},{3,0},{4,7},{5,6},{6,5},{7,4},{8,11},{9,10},{10,... | collective-permute-start | bytes 786440 | tf_op jit(solution)/shard_map/ppermute | solution.py:288
  69.8 28.8 %collective-permute-start.16 = (bf16[2,512,128]{2,1,0:T(8,128)(2,1)S(1)}, bf16[2,512,128]{2,1,0:T(8,128)(2,1)S(1)}, u32[]{:S(2)}, u32[]{:S(2)}) collective-permute-start(bf16[2,512,128]{2,1,0:T(8,128)(2,1)S(1)} %get-tuple-element.86), channel_id=1, source_target_pairs={{0,4},{1,5},{2,6},{3,7},{4,0},{5,1},{6,2},{7,3},{8,12},{9,13},{10,... | collective-permute-start | bytes 786440 | tf_op jit(solution)/shard_map/ppermute | solution.py:288
  75.1 118.7 %collective-permute-start.11 = (bf16[2,512,128]{2,1,0:T(8,128)(2,1)S(1)}, bf16[2,512,128]{2,1,0:T(8,128)(2,1)S(1)}, u32[]{:S(2)}, u32[]{:S(2)}) collective-permute-start(bf16[2,512,128]{2,1,0:T(8,128)(2,1)S(1)} %get-tuple-element.85), channel_id=1, source_target_pairs={{0,5},{1,4},{2,7},{3,6},{4,1},{5,0},{6,3},{7,2},{8,13},{9,12},{10,... | collective-permute-start | bytes 786440 | tf_op jit(solution)/shard_map/ppermute | solution.py:288
  80.2 113.6 %collective-permute-start.12 = (bf16[2,512,128]{2,1,0:T(8,128)(2,1)S(1)}, bf16[2,512,128]{2,1,0:T(8,128)(2,1)S(1)}, u32[]{:S(2)}, u32[]{:S(2)}) collective-permute-start(bf16[2,512,128]{2,1,0:T(8,128)(2,1)S(1)} %get-tuple-element.84), channel_id=1, source_target_pairs={{0,6},{1,7},{2,4},{3,5},{4,2},{5,3},{6,0},{7,1},{8,14},{9,15},{10,... | collective-permute-start | bytes 786440 | tf_op jit(solution)/shard_map/ppermute | solution.py:288
  94.6 113.7 %collective-permute-start.18 = (bf16[2,512,128]{2,1,0:T(8,128)(2,1)S(1)}, bf16[2,512,128]{2,1,0:T(8,128)(2,1)S(1)}, u32[]{:S(2)}, u32[]{:S(2)}) collective-permute-start(bf16[2,512,128]{2,1,0:T(8,128)(2,1)S(1)} %get-tuple-element.79), channel_id=1, source_target_pairs={{0,7},{1,6},{2,5},{3,4},{4,3},{5,2},{6,1},{7,0},{8,15},{9,14},{10,... | collective-permute-start | bytes 786440 | tf_op jit(solution)/shard_map/ppermute | solution.py:288
  118.5 89.0 %collective-permute-start.17 = (s32[1,2]{1,0:T(1,128)S(1)}, s32[1,2]{1,0:T(1,128)S(1)}, u32[]{:S(2)}, u32[]{:S(2)}) collective-permute-start(s32[1,2]{1,0:T(1,128)S(1)} %copy-done.12), channel_id=1, source_target_pairs={{0,488},{8,496},{64,40},{72,48},{128,104},{136,112},{192,168},{200... | collective-permute-start | bytes 32 | tf_op jit(solution)/shard_map/ppermute | solution.py:272
  216.5 5.3 %collective-permute-start.22 = (bf16[128,1152]{1,0:T(8,128)(2,1)}, bf16[128,1152]{1,0:T(8,128)(2,1)S(1)}, u32[]{:S(2)}, u32[]{:S(2)}) collective-permute-start(bf16[128,1152]{1,0:T(8,128)(2,1)} %get-tuple-element.73), channel_id=1, source_target_pairs={{56,40},{120,104},{184,168},{248,232},{312,296},{376,360},{440,424... | collective-permute-start | bytes 884744 | tf_op jit(solution)/shard_map/ppermute | solution.py:266
  217.1 6.0 %collective-permute-start.23 = (bf16[128,1152]{1,0:T(8,128)(2,1)}, bf16[128,1152]{1,0:T(8,128)(2,1)S(1)}, u32[]{:S(2)}, u32[]{:S(2)}) collective-permute-start(bf16[128,1152]{1,0:T(8,128)(2,1)} %get-tuple-element.74), channel_id=1, source_target_pairs={{48,40},{56,48},{112,104},{120,112},{176,168},{184,176},{240,232},... | collective-permute-start | bytes 884744 | tf_op jit(solution)/shard_map/ppermute | solution.py:266
  218.5 11.9 %collective-permute-start.19 = (bf16[128,1152]{1,0:T(8,128)(2,1)}, bf16[128,1152]{1,0:T(8,128)(2,1)S(1)}, u32[]{:S(2)}, u32[]{:S(2)}) collective-permute-start(bf16[128,1152]{1,0:T(8,128)(2,1)} %get-tuple-element.73), channel_id=1, source_target_pairs={{0,8},{8,16},{16,24},{24,32},{32,40},{40,48},{48,56},{64,72},{72,8... | collective-permute-start | bytes 884744 | tf_op jit(solution)/shard_map/ppermute | solution.py:266
  220.4 11.4 %collective-permute-start.20 = (bf16[128,1152]{1,0:T(8,128)(2,1)}, bf16[128,1152]{1,0:T(8,128)(2,1)S(1)}, u32[]{:S(2)}, u32[]{:S(2)}) collective-permute-start(bf16[128,1152]{1,0:T(8,128)(2,1)} %get-tuple-element.74), channel_id=1, source_target_pairs={{0,16},{8,24},{16,32},{24,40},{32,48},{40,56},{64,80},{72,88},{80,... | collective-permute-start | bytes 884744 | tf_op jit(solution)/shard_map/ppermute | solution.py:266
  221.8 15.3 %collective-permute-start.21 = (bf16[128,1152]{1,0:T(8,128)(2,1)}, bf16[128,1152]{1,0:T(8,128)(2,1)S(1)}, u32[]{:S(2)}, u32[]{:S(2)}) collective-permute-start(bf16[128,1152]{1,0:T(8,128)(2,1)} %get-tuple-element.75), channel_id=1, source_target_pairs={{0,24},{8,32},{16,40},{24,48},{32,56},{64,88},{72,96},{80,104},{88... | collective-permute-start | bytes 884744 | tf_op jit(solution)/shard_map/ppermute | solution.py:266
  224.2 25.5 %collective-permute-start.25 = (bf16[128,1152]{1,0:T(8,128)(2,1)S(1)}, bf16[128,1152]{1,0:T(8,128)(2,1)S(1)}, u32[]{:S(2)}, u32[]{:S(2)}) collective-permute-start(bf16[128,1152]{1,0:T(8,128)(2,1)S(1)} %select_select_fusion), channel_id=1, source_target_pairs={{40,64},{48,72},{16,80},{104,128},{112,136},{80,144},{168,192},{17... | collective-permute-start | bytes 884744 | tf_op jit(solution)/shard_map/ppermute | solution.py:272
  (15 other events, 133.1 us)

commit v3 on v1

--- a/solution.py
+++ b/solution.py
@@ -13,12 +13,13 @@
 STEPS = 4
 REACH = 4
 ROW = 8
+TAG = 16
 PART = 4
 HEADS = 8
 QROWS = 64
 MSG = HEADS * HD + 128
 MASKED = -1e30
-ORDER = ((0, 1, 2, 3), (4, 5, 6), (7,))
+ORDER = ((0, 1, 2, 3, 4, 5), (6, 7))
 SCALE2 = 1.4426950408889634 * HD ** (-0.5)
 
 
@@ -273,13 +274,17 @@
 
     caps = queries.shape[0]
     last_row = caps * QROWS
-    flat_q = queries.reshape(last_row, HEADS * HD)
-    hop = in_row(flat_q, [(1, 5)])
-    over = cross_row(jnp.where(place == 5, hop, flat_q), [(0, 0), (5, 5), (2, 2)], -1)
-    inside = [[(i, i - k) for i in range(k, ROW)] for k in range(1, REACH)]
-    tags = [in_row(offsets, inside[k - 1]) for k in range(1, REACH)]
-    far_offsets = cross_row(offsets, [(0, 5), (1, 6)], -1)
-    near = [in_row(flat_q, [(i, i - k) for i in range(k, ROW)]) for k in range(1, REACH)]
+    marks = jnp.repeat(offsets[0].astype(jnp.bfloat16), TAG // caps)
+    tagged = jnp.concatenate(
+        [
+            queries.reshape(last_row, HEADS * HD),
+            jnp.broadcast_to(marks[:, None], (TAG, HEADS * HD)),
+        ],
+        axis=0,
+    )
+    hop = in_row(tagged, [(1, 5)])
+    over = cross_row(jnp.where(place == 5, hop, tagged), [(0, 0), (5, 5), (2, 2)], -1)
+    near = [in_row(tagged, [(i, i - k) for i in range(k, ROW)]) for k in range(1, REACH)]
 
     def slab(j):
         return lax.dynamic_slice_in_dim(prompt_cache, (member ^ j) * HD, HD, 2)
@@ -295,23 +300,24 @@
     live = live_bias(block_table[0], lengths[0], member, members)
     biases = [jnp.concatenate([live[j] for j in order])[None, :] for order in ORDER]
     slots = REACH * caps
-    outside = [place + k >= ROW for k in range(1, REACH)]
-    wanted = jnp.concatenate(
-        [offsets[0] == 0] + [o | (t[0] == k) for k, (o, t) in enumerate(zip(outside, tags), 1)]
-    ).astype(jnp.int32)
-    q_all = jnp.stack([flat_q] + [jnp.where(o, f, n) for o, f, n in zip(outside, far, near)])
+    q_all = jnp.stack(
+        [tagged]
+        + [jnp.where(place + k >= ROW, far[k - 1], near[k - 1]) for k in range(1, REACH)]
+    )
+    asked = q_all[:, last_row::TAG // caps, 0].astype(jnp.int32)
+    wanted = (asked == jnp.arange(REACH, dtype=jnp.int32)[:, None]).astype(jnp.int32).reshape(-1)
     q_all, wanted, biases = lax.optimization_barrier((q_all, wanted, biases))
 
     state = flash_call(wanted, biases[0], q_all, [chunk[j] for j in ORDER[0]], None, (0, slots), caps)
-    state, later = lax.optimization_barrier((state, (queries, new_cache, far_offsets, offsets)))
-    own = own_call(*later[:2])
-    asked = later[2][0]
+    state, mine, asked, own_offsets = lax.optimization_barrier(
+        (state, (queries, new_cache), asked[3], offsets[0])
+    )
+    own = own_call(*mine)
     code = jnp.where(place == 2, 3, jnp.where(asked == 3, 0, asked))
     pick = jnp.broadcast_to(jnp.repeat(code, QROWS)[:, None], (last_row, HD))
-    source = jnp.where(later[3][0] <= place, later[3][0], REACH)
+    source = jnp.where(own_offsets <= place, own_offsets, REACH)
     state, own, pick, source = lax.optimization_barrier((state, own, pick, source))
-    state = flash_call(wanted, biases[1], q_all, [chunk[j] for j in ORDER[1]], state, (0, slots), caps)
-    final = partial(flash_call, wanted, biases[2], q_all, [chunk[j] for j in ORDER[2]], state)
+    final = partial(flash_call, wanted, biases[1], q_all, [chunk[j] for j in ORDER[1]], state)
     message = [None, *final((caps, slots - caps), caps, True)]
 
     gathered = [

time: 239 us -> 207 us (0.87)
  the two profiles are of different devices: /device:TPU:33 before, /device:TPU:97 now
where the time goes in v3:
time: 207 us; the launch traced here: 206 us
  starting transfers between devices  90.5 us (44%)
  waiting for transfers between devices  63.6 us (31%)
  Pallas kernels  38 us (18%)
  other arithmetic  7.31 us (4%)
  local copies, waits for them, and re-layouts  5.3 us (3%)
    ppermute x13, starting transfers between devices, in_row(): return lax.ppermute(value, 'group', whole)  58.1 us
    ppermute x7, waiting for transfers between devices, exchanged(): return lax.ppermute(value, 'tensor', [(m, m ^ j) for m in range(members)])  39.3 us
    pallas_call x3, Pallas kernels, flash_call(): pl.pallas_call(partial(flash_kernel, n, lo, first, caps if last else None...  32.2 us
    ppermute x7, starting transfers between devices, exchanged(): return lax.ppermute(value, 'tensor', [(m, m ^ j) for m in range(members)])  29.7 us
    ppermute x2, waiting for transfers between devices, cross_row(): return lax.ppermute(value, 'group', whole)  23.7 us
  transfers between devices with their start and end apart: 22, of which 6 were waited for; matrix products, arithmetic and copies ran while one was open for 4% of the time, Pallas kernels for 13%

profile of v3, /device:TPU:97, one launch (start us, length us, event | category | flops | bytes accessed | tf_op | source)
XLA Modules:
  0.0 205.9 jit_solution(6045720734787944425)
XLA Ops:
  1.9 2.6 %collective-permute-start.3 = (bf16[144,1024]{1,0:T(8,128)(2,1)S(1)}, bf16[144,1024]{1,0:T(8,128)(2,1)S(1)}, u32[]{:S(2)}, u32[]{:S(2)}) collective-permute-start(bf16[144,1024]{1,0:T(8,128)(2,1)S(1)} %pad_maximum_fusion.1), channel_id=1, source_target_pairs={{8,0},{16,8},{24,16},{32,24},{40,32},{48,40},{56,48},{72,64},{80,7... | collective-permute-start | bytes 884744 | tf_op jit(solution)/shard_map/ppermute | solution.py:267
  5.8 5.4 %collective-permute-start = (bf16[144,1024]{1,0:T(8,128)(2,1)S(1)}, bf16[144,1024]{1,0:T(8,128)(2,1)S(1)}, u32[]{:S(2)}, u32[]{:S(2)}) collective-permute-start(bf16[144,1024]{1,0:T(8,128)(2,1)S(1)} %pad_maximum_fusion.1), channel_id=1, source_target_pairs={{8,40},{72,104},{136,168},{200,232},{264,296},{328,360},{392,424},... | collective-permute-start | bytes 884744 | tf_op jit(solution)/shard_map/ppermute | solution.py:267
  16.0 1.4 collective-permute-start.1
  18.1 2.5 %constant_dynamic-slice_fusion = (bf16[2,512,128]{2,1,0:T(8,128)(2,1)S(1)}, bf16[2,512,128]{2,1,0:T(8,128)(2,1)}, bf16[2,512,128]{2,1,0:T(8,128)(2,1)}, bf16[2,5...) fusion(bf16[2,512,1024]{2,1,0:T(8,128)(2,1)} %param.6, ...), kind=kLoop, calls=%fused_computation.29 | loop fusion | bytes 4194336 | tf_op jit(solution)/shard_map/dynamic_slice | solution.py:290
  22.0 7.5 %collective-permute-start.12 = (bf16[2,512,128]{2,1,0:T(8,128)(2,1)}, bf16[2,512,128]{2,1,0:T(8,128)(2,1)}, u32[]{:S(2)}, u32[]{:S(2)}) collective-permute-start(bf16[2,512,128]{2,1,0:T(8,128)(2,1)} %get-tuple-element.52), channel_id=1, source_target_pairs={{0,5},{1,4},{2,7},{3,6},{4,1},{5,0},{6,3},{7,2},{8,13},{9,12},{10,... | collective-permute-start | bytes 786440 | tf_op jit(solution)/shard_map/ppermute | solution.py:294
  30.2 3.3 %collective-permute-start.11 = (bf16[2,512,128]{2,1,0:T(8,128)(2,1)}, bf16[2,512,128]{2,1,0:T(8,128)(2,1)}, u32[]{:S(2)}, u32[]{:S(2)}) collective-permute-start(bf16[2,512,128]{2,1,0:T(8,128)(2,1)} %get-tuple-element.53), channel_id=1, source_target_pairs={{0,4},{1,5},{2,6},{3,7},{4,0},{5,1},{6,2},{7,3},{8,12},{9,13},{10,... | collective-permute-start | bytes 786440 | tf_op jit(solution)/shard_map/ppermute | solution.py:294
  33.5 2.2 %collective-permute-start.10 = (bf16[2,512,128]{2,1,0:T(8,128)(2,1)S(1)}, bf16[2,512,128]{2,1,0:T(8,128)(2,1)}, u32[]{:S(2)}, u32[]{:S(2)}) collective-permute-start(bf16[2,512,128]{2,1,0:T(8,128)(2,1)S(1)} %get-tuple-element.54), channel_id=1, source_target_pairs={{0,3},{1,2},{2,1},{3,0},{4,7},{5,6},{6,5},{7,4},{8,11},{9,10},{10,... | collective-permute-start | bytes 786440 | tf_op jit(solution)/shard_map/ppermute | solution.py:294
  35.8 4.0 %collective-permute-start.9 = (bf16[2,512,128]{2,1,0:T(8,128)(2,1)S(1)}, bf16[2,512,128]{2,1,0:T(8,128)(2,1)}, u32[]{:S(2)}, u32[]{:S(2)}) collective-permute-start(bf16[2,512,128]{2,1,0:T(8,128)(2,1)S(1)} %get-tuple-element.55), channel_id=1, source_target_pairs={{0,2},{1,3},{2,0},{3,1},{4,6},{5,7},{6,4},{7,5},{8,10},{9,11},{10,... | collective-permute-start | bytes 786440 | tf_op jit(solution)/shard_map/ppermute | solution.py:294
  39.8 3.1 %collective-permute-start.8 = (bf16[2,512,128]{2,1,0:T(8,128)(2,1)S(1)}, bf16[2,512,128]{2,1,0:T(8,128)(2,1)}, u32[]{:S(2)}, u32[]{:S(2)}) collective-permute-start(bf16[2,512,128]{2,1,0:T(8,128)(2,1)S(1)} %get-tuple-element.56), channel_id=1, source_target_pairs={{0,1},{1,0},{2,3},{3,2},{4,5},{5,4},{6,7},{7,6},{8,9},{9,8},{10,11... | collective-permute-start | bytes 786440 | tf_op jit(solution)/shard_map/ppermute | solution.py:294
  44.1 6.1 %collective-permute-done.12.refs_5_ = bf16[2,512,128]{2,1,0:T(8,128)(2,1)} collective-permute-done((bf16[2,512,128]{2,1,0:T(8,128)(2,1)}, bf16[2,512,128]{2,1,0:T(8,128)(2,1)}, u32[]{:S(2)}, u32[]{:S(2)}) %collective-permute-start.12) | collective-permute-done | bytes 262176 | tf_op jit(solution)/shard_map/ppermute | solution.py:294
  50.1 5.8 %collective-permute-start.14 = (bf16[2,512,128]{2,1,0:T(8,128)(2,1)S(1)}, bf16[2,512,128]{2,1,0:T(8,128)(2,1)S(1)}, u32[]{:S(2)}, u32[]{:S(2)}) collective-permute-start(bf16[2,512,128]{2,1,0:T(8,128)(2,1)S(1)} %get-tuple-element.51), channel_id=1, source_target_pairs={{0,7},{1,6},{2,5},{3,4},{4,3},{5,2},{6,1},{7,0},{8,15},{9,14},{10,... | collective-permute-start | bytes 786440 | tf_op jit(solution)/shard_map/ppermute | solution.py:294
  55.9 3.4 %collective-permute-done.11.refs_4_ = bf16[2,512,128]{2,1,0:T(8,128)(2,1)} collective-permute-done((bf16[2,512,128]{2,1,0:T(8,128)(2,1)}, bf16[2,512,128]{2,1,0:T(8,128)(2,1)}, u32[]{:S(2)}, u32[]{:S(2)}) %collective-permute-start.11) | collective-permute-done | bytes 262176 | tf_op jit(solution)/shard_map/ppermute | solution.py:294
  59.3 4.0 %collective-permute-start.13 = (bf16[2,512,128]{2,1,0:T(8,128)(2,1)S(1)}, bf16[2,512,128]{2,1,0:T(8,128)(2,1)S(1)}, u32[]{:S(2)}, u32[]{:S(2)}) collective-permute-start(bf16[2,512,128]{2,1,0:T(8,128)(2,1)S(1)} %get-tuple-element.58), channel_id=1, source_target_pairs={{0,6},{1,7},{2,4},{3,5},{4,2},{5,3},{6,0},{7,1},{8,14},{9,15},{10,... | collective-permute-start | bytes 786440 | tf_op jit(solution)/shard_map/ppermute | solution.py:294
  63.3 7.8 %collective-permute-done.9.refs_2_ = bf16[2,512,128]{2,1,0:T(8,128)(2,1)} collective-permute-done((bf16[2,512,128]{2,1,0:T(8,128)(2,1)S(1)}, bf16[2,512,128]{2,1,0:T(8,128)(2,1)}, u32[]{:S(2)}, u32[]{:S(2)}) %collective-permute-start.9) | collective-permute-done | bytes 262176 | tf_op jit(solution)/shard_map/ppermute | solution.py:294
  71.1 22.1 %collective-permute-done.8.refs_1_ = bf16[2,512,128]{2,1,0:T(8,128)(2,1)} collective-permute-done((bf16[2,512,128]{2,1,0:T(8,128)(2,1)S(1)}, bf16[2,512,128]{2,1,0:T(8,128)(2,1)}, u32[]{:S(2)}, u32[]{:S(2)}) %collective-permute-start.8) | collective-permute-done | bytes 262176 | tf_op jit(solution)/shard_map/ppermute | solution.py:294
  93.2 18.2 %flash_part.1 = (f32[8,512,256]{2,1,0:T(8,128)}, f32[8,512,128]{2,1,0:T(8,128)}) custom-call(s32[8]{0:T(128)} %compare_convert_fusion.wanted_ref, f32[1,3072]{1,0:T(1,128)} %bitcast.56, bf16[4,144,1024]{2,1,0:T(8,128)(2,1)} %copy-done, bf16[2,512,128]{2,1,0:T(8,128)(2,1)} %get-tuple-element.57.refs_0_, bf16[2,512,128]{2,1,0:T(8,128)(2,1)} %collective-permute-done.8.refs_1_, ...), custom_call_target="tpu_custom_call" | custom-call | flops 12884901888 | bytes 1572864 | tf_op jit(solution)/shard_map/flash_part/pallas_call | solution.py:134
  112.2 2.5 %own_part.1 = (f32[2,64,1024]{2,1,0:T(8,128)}, f32[2,64,128]{2,1,0:T(8,128)}) custom-call(bf16[2,64,1024]{2,1,0:T(8,128)(2,1)} %q_ref, bf16[2,2,64,128]{3,2,1,0:T(8,128)(2,1)} %new_ref), custom_call_target="tpu_custom_call" | custom-call | tf_op jit(solution)/shard_map/own_part/pallas_call | solution.py:182
  116.1 8.4 %flash_last.3 = (bf16[128,1152]{1,0:T(8,128)(2,1)}, bf16[128,1152]{1,0:T(8,128)(2,1)}, bf16[128,1152]{1,0:T(8,128)(2,1)}) custom-call(s32[8]{0:T(128)} %compare_convert_fusion.wanted_ref, f32[1,1024]{1,0:T(1,128)} %bitcast.52, bf16[4,144,1024]{2,1,0:T(8,128)(2,1)} %copy-done, bf16[2,512,128]{2,1,0:T(8,128)(2,1)} %copy-done.6, ...), custom_call_target="tpu_custom_call" | custom-call | flops 3221225472 | bytes 524288 | tf_op jit(solution)/shard_map/flash_last/pallas_call | solution.py:134
  126.6 18.0 %collective-permute-start.15 = (bf16[128,1152]{1,0:T(8,128)(2,1)}, bf16[128,1152]{1,0:T(8,128)(2,1)S(1)}, u32[]{:S(2)}, u32[]{:S(2)}) collective-permute-start(bf16[128,1152]{1,0:T(8,128)(2,1)} %get-tuple-element.45), channel_id=1, source_target_pairs={{0,8},{8,16},{16,24},{24,32},{32,40},{40,48},{48,56},{64,72},{72,8... | collective-permute-start | bytes 884744 | tf_op jit(solution)/shard_map/ppermute | solution.py:267
  144.6 1.3 collective-permute-start.16
  145.9 24.1 %collective-permute-start.17 = (bf16[128,1152]{1,0:T(8,128)(2,1)}, bf16[128,1152]{1,0:T(8,128)(2,1)S(1)}, u32[]{:S(2)}, u32[]{:S(2)}) collective-permute-start(bf16[128,1152]{1,0:T(8,128)(2,1)} %get-tuple-element.47), channel_id=1, source_target_pairs={{0,24},{8,32},{16,40},{24,48},{32,56},{64,88},{72,96},{80,104},{88... | collective-permute-start | bytes 884744 | tf_op jit(solution)/shard_map/ppermute | solution.py:267
  172.5 5.6 %flash_last.2.m0 = bf16[128,1152]{1,0:T(8,128)(2,1)} custom-call(s32[8]{0:T(128)} %compare_convert_fusion.wanted_ref, f32[1,1024]{1,0:T(1,128)} %bitcast.53, bf16[4,144,1024]{2,1,0:T(8,128)(2,1)} %copy-done, bf16[2,512,128]{2,1,0:T(8,128)(2,1)} %copy-done.6, bf16[2,512,128]{2,1,0:T(8,128)(2,1)} %copy-done.5, f32[8,512,256]{2,1,0:T(8,128)} %get-tuple-element.43.refs_2_, ...), custom_call_target="tpu_custom_call" | custom-call | flops 1073741824 | bytes 524288 | tf_op jit(solution)/shard_map/flash_last/pallas_call | solution.py:134
  178.2 23.7 %collective-permute-done.21.m4 = bf16[128,1152]{1,0:T(8,128)(2,1)S(1)} collective-permute-done((bf16[128,1152]{1,0:T(8,128)(2,1)S(1)}, bf16[128,1152]{1,0:T(8,128)(2,1)S(1)}, u32[]{:S(2)}, u32[]{:S(2)}) %collective-permute-start.21) | collective-permute-done | bytes 294944 | tf_op jit(solution)/shard_map/ppermute | solution.py:273
  202.6 3.3 %merge.1 = bf16[2,64,1024]{2,1,0:T(8,128)(2,1)} custom-call(s32[2]{0:T(128)} %get-tuple-element.41.code_ref, bf16[128,1152]{1,0:T(8,128)(2,1)} %flash_last.2.m0, bf16[128,1152]{1,0:T(8,128)(2,1)} %copy-done.1, bf16[128,1152]{1,0:T(8,128)(2,1)} %copy-done.2, bf16[128,1152]{1,0:T(8,128)(2,1)} %copy-done.3, bf16[128,1152]{1,0:T(8,128)(2,1)} %copy-done.4, ...), custom_call_target="tpu_custom_call" | custom-call | tf_op jit(solution)/shard_map/merge/pallas_call | solution.py:227
  (82 shorter events, 18.6 us)
Async XLA Ops:
  1.9 28.3 %collective-permute-start.3 = (bf16[144,1024]{1,0:T(8,128)(2,1)S(1)}, bf16[144,1024]{1,0:T(8,128)(2,1)S(1)}, u32[]{:S(2)}, u32[]{:S(2)}) collective-permute-start(bf16[144,1024]{1,0:T(8,128)(2,1)S(1)} %pad_maximum_fusion.1), channel_id=1, source_target_pairs={{8,0},{16,8},{24,16},{32,24},{40,32},{48,40},{56,48},{72,64},{80,7... | collective-permute-start | bytes 884744 | tf_op jit(solution)/shard_map/ppermute | solution.py:267
  4.5 17.5 %collective-permute-start.7 = (bf16[144,1024]{1,0:T(8,128)(2,1)S(1)}, bf16[144,1024]{1,0:T(8,128)(2,1)S(1)}, u32[]{:S(2)}, u32[]{:S(2)}) collective-permute-start(bf16[144,1024]{1,0:T(8,128)(2,1)S(1)} %pad_maximum_fusion.1), channel_id=1, source_target_pairs={{24,0},{32,8},{40,16},{48,24},{56,32},{88,64},{96,72},{104,80},{11... | collective-permute-start | bytes 884744 | tf_op jit(solution)/shard_map/ppermute | solution.py:267
  5.8 9.1 %collective-permute-start = (bf16[144,1024]{1,0:T(8,128)(2,1)S(1)}, bf16[144,1024]{1,0:T(8,128)(2,1)S(1)}, u32[]{:S(2)}, u32[]{:S(2)}) collective-permute-start(bf16[144,1024]{1,0:T(8,128)(2,1)S(1)} %pad_maximum_fusion.1), channel_id=1, source_target_pairs={{8,40},{72,104},{136,168},{200,232},{264,296},{328,360},{392,424},... | collective-permute-start | bytes 884744 | tf_op jit(solution)/shard_map/ppermute | solution.py:267
  11.2 24.5 %collective-permute-start.5 = (bf16[144,1024]{1,0:T(8,128)(2,1)S(1)}, bf16[144,1024]{1,0:T(8,128)(2,1)S(1)}, u32[]{:S(2)}, u32[]{:S(2)}) collective-permute-start(bf16[144,1024]{1,0:T(8,128)(2,1)S(1)} %pad_maximum_fusion.1), channel_id=1, source_target_pairs={{16,0},{24,8},{32,16},{40,24},{48,32},{56,40},{80,64},{88,72},{96,... | collective-permute-start | bytes 884744 | tf_op jit(solution)/shard_map/ppermute | solution.py:267
  16.0 1.4 collective-permute-start.1
  17.4 12.1 %collective-permute-start.6 = (bf16[144,1024]{1,0:T(8,128)(2,1)}, bf16[144,1024]{1,0:T(8,128)(2,1)S(1)}, u32[]{:S(2)}, u32[]{:S(2)}) collective-permute-start(bf16[144,1024]{1,0:T(8,128)(2,1)} %collective-permute-done.1), channel_id=1, source_target_pairs={{0,40},{40,48},{16,56},{64,104},{104,112},{80,120},{128,168},{168,... | collective-permute-start | bytes 884744 | tf_op jit(solution)/shard_map/ppermute | solution.py:267
  20.7 12.9 %collective-permute-start.2 = (bf16[144,1024]{1,0:T(8,128)(2,1)}, bf16[144,1024]{1,0:T(8,128)(2,1)S(1)}, u32[]{:S(2)}, u32[]{:S(2)}) collective-permute-start(bf16[144,1024]{1,0:T(8,128)(2,1)} %collective-permute-done.1), channel_id=1, source_target_pairs={{0,56},{64,120},{128,184},{192,248},{256,312},{320,376},{384,440},... | collective-permute-start | bytes 884744 | tf_op jit(solution)/shard_map/ppermute | solution.py:267
  22.0 28.1 %collective-permute-start.12 = (bf16[2,512,128]{2,1,0:T(8,128)(2,1)}, bf16[2,512,128]{2,1,0:T(8,128)(2,1)}, u32[]{:S(2)}, u32[]{:S(2)}) collective-permute-start(bf16[2,512,128]{2,1,0:T(8,128)(2,1)} %get-tuple-element.52), channel_id=1, source_target_pairs={{0,5},{1,4},{2,7},{3,6},{4,1},{5,0},{6,3},{7,2},{8,13},{9,12},{10,... | collective-permute-start | bytes 786440 | tf_op jit(solution)/shard_map/ppermute | solution.py:294
  29.5 10.3 %collective-permute-start.4 = (bf16[144,1024]{1,0:T(8,128)(2,1)}, bf16[144,1024]{1,0:T(8,128)(2,1)S(1)}, u32[]{:S(2)}, u32[]{:S(2)}) collective-permute-start(bf16[144,1024]{1,0:T(8,128)(2,1)} %collective-permute-done.1), channel_id=1, source_target_pairs={{0,48},{40,56},{64,112},{104,120},{128,176},{168,184},{192,240},{2... | collective-permute-start | bytes 884744 | tf_op jit(solution)/shard_map/ppermute | solution.py:267
  30.2 29.1 %collective-permute-start.11 = (bf16[2,512,128]{2,1,0:T(8,128)(2,1)}, bf16[2,512,128]{2,1,0:T(8,128)(2,1)}, u32[]{:S(2)}, u32[]{:S(2)}) collective-permute-start(bf16[2,512,128]{2,1,0:T(8,128)(2,1)} %get-tuple-element.53), channel_id=1, source_target_pairs={{0,4},{1,5},{2,6},{3,7},{4,0},{5,1},{6,2},{7,3},{8,12},{9,13},{10,... | collective-permute-start | bytes 786440 | tf_op jit(solution)/shard_map/ppermute | solution.py:294
  33.5 29.8 %collective-permute-start.10 = (bf16[2,512,128]{2,1,0:T(8,128)(2,1)S(1)}, bf16[2,512,128]{2,1,0:T(8,128)(2,1)}, u32[]{:S(2)}, u32[]{:S(2)}) collective-permute-start(bf16[2,512,128]{2,1,0:T(8,128)(2,1)S(1)} %get-tuple-element.54), channel_id=1, source_target_pairs={{0,3},{1,2},{2,1},{3,0},{4,7},{5,6},{6,5},{7,4},{8,11},{9,10},{10,... | collective-permute-start | bytes 786440 | tf_op jit(solution)/shard_map/ppermute | solution.py:294
  35.8 35.3 %collective-permute-start.9 = (bf16[2,512,128]{2,1,0:T(8,128)(2,1)S(1)}, bf16[2,512,128]{2,1,0:T(8,128)(2,1)}, u32[]{:S(2)}, u32[]{:S(2)}) collective-permute-start(bf16[2,512,128]{2,1,0:T(8,128)(2,1)S(1)} %get-tuple-element.55), channel_id=1, source_target_pairs={{0,2},{1,3},{2,0},{3,1},{4,6},{5,7},{6,4},{7,5},{8,10},{9,11},{10,... | collective-permute-start | bytes 786440 | tf_op jit(solution)/shard_map/ppermute | solution.py:294
  39.8 53.4 %collective-permute-start.8 = (bf16[2,512,128]{2,1,0:T(8,128)(2,1)S(1)}, bf16[2,512,128]{2,1,0:T(8,128)(2,1)}, u32[]{:S(2)}, u32[]{:S(2)}) collective-permute-start(bf16[2,512,128]{2,1,0:T(8,128)(2,1)S(1)} %get-tuple-element.56), channel_id=1, source_target_pairs={{0,1},{1,0},{2,3},{3,2},{4,5},{5,4},{6,7},{7,6},{8,9},{9,8},{10,11... | collective-permute-start | bytes 786440 | tf_op jit(solution)/shard_map/ppermute | solution.py:294
  43.1 50.1 %copy-start = (bf16[4,144,1024]{2,1,0:T(8,128)(2,1)}, bf16[4,144,1024]{2,1,0:T(8,128)(2,1)S(1)}, u32[]{:S(2)}) copy-start(bf16[4,144,1024]{2,1,0:T(8,128)(2,1)S(1)} %pad_maximum_fusion.q_ref) | copy-start | bytes 3538948
  50.1 64.6 %collective-permute-start.14 = (bf16[2,512,128]{2,1,0:T(8,128)(2,1)S(1)}, bf16[2,512,128]{2,1,0:T(8,128)(2,1)S(1)}, u32[]{:S(2)}, u32[]{:S(2)}) collective-permute-start(bf16[2,512,128]{2,1,0:T(8,128)(2,1)S(1)} %get-tuple-element.51), channel_id=1, source_target_pairs={{0,7},{1,6},{2,5},{3,4},{4,3},{5,2},{6,1},{7,0},{8,15},{9,14},{10,... | collective-permute-start | bytes 786440 | tf_op jit(solution)/shard_map/ppermute | solution.py:294
  59.3 55.4 %collective-permute-start.13 = (bf16[2,512,128]{2,1,0:T(8,128)(2,1)S(1)}, bf16[2,512,128]{2,1,0:T(8,128)(2,1)S(1)}, u32[]{:S(2)}, u32[]{:S(2)}) collective-permute-start(bf16[2,512,128]{2,1,0:T(8,128)(2,1)S(1)} %get-tuple-element.58), channel_id=1, source_target_pairs={{0,6},{1,7},{2,4},{3,5},{4,2},{5,3},{6,0},{7,1},{8,14},{9,15},{10,... | collective-permute-start | bytes 786440 | tf_op jit(solution)/shard_map/ppermute | solution.py:294
  124.5 21.4 %collective-permute-start.18 = (bf16[128,1152]{1,0:T(8,128)(2,1)}, bf16[128,1152]{1,0:T(8,128)(2,1)S(1)}, u32[]{:S(2)}, u32[]{:S(2)}) collective-permute-start(bf16[128,1152]{1,0:T(8,128)(2,1)} %get-tuple-element.45), channel_id=1, source_target_pairs={{56,40},{120,104},{184,168},{248,232},{312,296},{376,360},{440,424... | collective-permute-start | bytes 884744 | tf_op jit(solution)/shard_map/ppermute | solution.py:267
  125.2 44.9 %collective-permute-start.19 = (bf16[128,1152]{1,0:T(8,128)(2,1)}, bf16[128,1152]{1,0:T(8,128)(2,1)S(1)}, u32[]{:S(2)}, u32[]{:S(2)}) collective-permute-start(bf16[128,1152]{1,0:T(8,128)(2,1)} %get-tuple-element.46), channel_id=1, source_target_pairs={{48,40},{56,48},{112,104},{120,112},{176,168},{184,176},{240,232},... | collective-permute-start | bytes 884744 | tf_op jit(solution)/shard_map/ppermute | solution.py:267
  125.9 44.2 %collective-permute-start.20 = (bf16[128,1152]{1,0:T(8,128)(2,1)}, bf16[128,1152]{1,0:T(8,128)(2,1)S(1)}, u32[]{:S(2)}, u32[]{:S(2)}) collective-permute-start(bf16[128,1152]{1,0:T(8,128)(2,1)} %get-tuple-element.47), channel_id=1, source_target_pairs={{56,16},{120,80},{184,144},{248,208},{312,272},{376,336},{440,400}... | collective-permute-start | bytes 884744 | tf_op jit(solution)/shard_map/ppermute | solution.py:267
  126.6 51.5 %collective-permute-start.15 = (bf16[128,1152]{1,0:T(8,128)(2,1)}, bf16[128,1152]{1,0:T(8,128)(2,1)S(1)}, u32[]{:S(2)}, u32[]{:S(2)}) collective-permute-start(bf16[128,1152]{1,0:T(8,128)(2,1)} %get-tuple-element.45), channel_id=1, source_target_pairs={{0,8},{8,16},{16,24},{24,32},{32,40},{40,48},{48,56},{64,72},{72,8... | collective-permute-start | bytes 884744 | tf_op jit(solution)/shard_map/ppermute | solution.py:267
  144.6 33.5 %collective-permute-start.16 = (bf16[128,1152]{1,0:T(8,128)(2,1)}, bf16[128,1152]{1,0:T(8,128)(2,1)S(1)}, u32[]{:S(2)}, u32[]{:S(2)}) collective-permute-start(bf16[128,1152]{1,0:T(8,128)(2,1)} %get-tuple-element.46), channel_id=1, source_target_pairs={{0,16},{8,24},{16,32},{24,40},{32,48},{40,56},{64,80},{72,88},{80,... | collective-permute-start | bytes 884744 | tf_op jit(solution)/shard_map/ppermute | solution.py:267
  145.9 32.2 %collective-permute-start.17 = (bf16[128,1152]{1,0:T(8,128)(2,1)}, bf16[128,1152]{1,0:T(8,128)(2,1)S(1)}, u32[]{:S(2)}, u32[]{:S(2)}) collective-permute-start(bf16[128,1152]{1,0:T(8,128)(2,1)} %get-tuple-element.47), channel_id=1, source_target_pairs={{0,24},{8,32},{16,40},{24,48},{32,56},{64,88},{72,96},{80,104},{88... | collective-permute-start | bytes 884744 | tf_op jit(solution)/shard_map/ppermute | solution.py:267
  171.2 30.7 %collective-permute-start.21 = (bf16[128,1152]{1,0:T(8,128)(2,1)S(1)}, bf16[128,1152]{1,0:T(8,128)(2,1)S(1)}, u32[]{:S(2)}, u32[]{:S(2)}) collective-permute-start(bf16[128,1152]{1,0:T(8,128)(2,1)S(1)} %select_select_fusion), channel_id=1, source_target_pairs={{40,64},{48,72},{16,80},{104,128},{112,136},{80,144},{168,192},{17... | collective-permute-start | bytes 884744 | tf_op jit(solution)/shard_map/ppermute | solution.py:273
  178.1 23.8 %copy-start.1 = (bf16[128,1152]{1,0:T(8,128)(2,1)}, bf16[128,1152]{1,0:T(8,128)(2,1)S(1)}, u32[]{:S(2)}) copy-start(bf16[128,1152]{1,0:T(8,128)(2,1)S(1)} %collective-permute-done.15.m1) | copy-start | bytes 884740
  (7 other events, 70.5 us)

commit v4 on v3

--- a/solution.py
+++ b/solution.py
@@ -19,7 +19,7 @@
 QROWS = 64
 MSG = HEADS * HD + 128
 MASKED = -1e30
-ORDER = ((0, 1, 2, 3, 4, 5), (6, 7))
+ORDER = ((0, 1, 4, 2), (5, 3, 6), (7,))
 SCALE2 = 1.4426950408889634 * HD ** (-0.5)
 
 
@@ -189,11 +189,11 @@
     )(queries, new_cache)
 
 
-def merge_kernel(code_ref, m0, m1, m2, m3, m4, part_ref, stat_ref, out_ref, msg, sem):
+def merge_kernel(code_ref, m0, m1, m2, m3, m4, m5, part_ref, stat_ref, out_ref, msg, sem):
     slots = out_ref.shape[0]
     for slot in range(slots):
         rows = pl.ds(slot * QROWS, QROWS)
-        for index, ref in enumerate((m0, m1, m2, m3, m4)):
+        for index, ref in enumerate((m0, m1, m2, m3, m4, m5)):
 
             @pl.when(code_ref[slot] == index)
             def _():
@@ -226,7 +226,7 @@
     anywhere = pl.BlockSpec(memory_space=pltpu.HBM)
     return pl.pallas_call(
         merge_kernel,
-        in_specs=[pl.BlockSpec(memory_space=pltpu.SMEM)] + [anywhere] * 5 + [vmem] * 2,
+        in_specs=[pl.BlockSpec(memory_space=pltpu.SMEM)] + [anywhere] * 6 + [vmem] * 2,
         out_specs=vmem,
         out_shape=jax.ShapeDtypeStruct(shape, jnp.bfloat16),
         scratch_shapes=[
@@ -313,28 +313,21 @@
         (state, (queries, new_cache), asked[3], offsets[0])
     )
     own = own_call(*mine)
-    code = jnp.where(place == 2, 3, jnp.where(asked == 3, 0, asked))
-    pick = jnp.broadcast_to(jnp.repeat(code, QROWS)[:, None], (last_row, HD))
-    source = jnp.where(own_offsets <= place, own_offsets, REACH)
+    pick = jnp.broadcast_to(jnp.repeat(asked, QROWS)[:, None], (last_row, HD))
+    source = jnp.where(own_offsets <= place, own_offsets, jnp.where(place == 2, REACH + 1, REACH))
     state, own, pick, source = lax.optimization_barrier((state, own, pick, source))
-    final = partial(flash_call, wanted, biases[1], q_all, [chunk[j] for j in ORDER[1]], state)
+    state = flash_call(wanted, biases[1], q_all, [chunk[j] for j in ORDER[1]], state, (0, slots), caps)
+    final = partial(flash_call, wanted, biases[2], q_all, [chunk[j] for j in ORDER[2]], state)
     message = [None, *final((caps, slots - caps), caps, True)]
 
-    gathered = [
-        in_row(message[1], [(7, 5)]),
-        in_row(message[2], [(6, 5), (7, 6)]),
-        in_row(message[3], [(7, 2)]),
-    ]
+    gathered = [in_row(message[1], [(7, 5)]), in_row(message[2], [(6, 5), (7, 6)])]
+    direct = cross_row(message[3], [(7, 2)], 1)
     back = [in_row(message[k], [(i, i + k) for i in range(ROW - k)]) for k in range(1, REACH)]
     pick = pick[:, :1]
-    passed = jnp.where(
-        pick == 1,
-        gathered[0],
-        jnp.where(pick == 2, gathered[1], jnp.where(pick == 3, gathered[2], message[3])),
-    )
-    crossed = cross_row(passed, [(5, 0), (6, 1), (2, 2)], 1)
+    passed = jnp.where(pick == 1, gathered[0], jnp.where(pick == 2, gathered[1], message[3]))
+    crossed = cross_row(passed, [(5, 0), (6, 1)], 1)
     (message[0],) = final((0, caps), caps, True)
-    return merge_call(source, [message[0], *back, crossed], own, queries.shape)
+    return merge_call(source, [message[0], *back, crossed, direct], own, queries.shape)
 
 
 def solution(mesh):

time: 207 us -> 225 us (1.087)
  waiting for transfers between devices: 63.6 us -> 90.6 us
  starting transfers between devices: 90.5 us -> 72.6 us
  Pallas kernels: 38 us -> 46.6 us
    ppermute x7, waiting for transfers between devices: 39.3 us -> 65.9 us  [exchanged(): return lax.ppermute(value, 'tensor', [(m, m ^ j) for m in range(members)])]
    ppermute x13 -> x12, starting transfers between devices: 58.1 us -> 41.2 us  [in_row(): return lax.ppermute(value, 'group', whole)]
    pallas_call x3 -> x4, Pallas kernels: 32.2 us -> 40.8 us  [flash_call(): pl.pallas_call(partial(flash_kernel, n, lo, first, caps if last else None...]
    ppermute x2 -> x3, waiting for transfers between devices: 23.7 us -> 24 us  [cross_row(): return lax.ppermute(value, 'group', whole)]
  transfers between devices with their start and end apart: 22 -> 22, of which waited for: 6 -> 4; matrix products, arithmetic and copies ran while one was open for 4% -> 4% of each run, Pallas kernels for 13% -> 16%
where the time goes in v4:
time: 225 us; the launch traced here: 224 us
  waiting for transfers between devices  90.6 us (40%)
  starting transfers between devices  72.6 us (32%)
  Pallas kernels  46.6 us (21%)
  other arithmetic  7.26 us (3%)
  local copies, waits for them, and re-layouts  5.78 us (3%)
    ppermute x7, waiting for transfers between devices, exchanged(): return lax.ppermute(value, 'tensor', [(m, m ^ j) for m in range(members)])  65.9 us
    ppermute x12, starting transfers between devices, in_row(): return lax.ppermute(value, 'group', whole)  41.2 us
    pallas_call x4, Pallas kernels, flash_call(): pl.pallas_call(partial(flash_kernel, n, lo, first, caps if last else None...  40.8 us
    ppermute x7, starting transfers between devices, exchanged(): return lax.ppermute(value, 'tensor', [(m, m ^ j) for m in range(members)])  28 us
    ppermute x3, waiting for transfers between devices, cross_row(): return lax.ppermute(value, 'group', whole)  24 us
  transfers between devices with their start and end apart: 22, of which 4 were waited for; matrix products, arithmetic and copies ran while one was open for 4% of the time, Pallas kernels for 16%

profile of v4, /device:TPU:97, one launch (start us, length us, event | category | flops | bytes accessed | tf_op | source)
XLA Modules:
  0.0 224.0 jit_solution(17161438318944574541)
XLA Ops:
  1.9 2.6 %collective-permute-start.3 = (bf16[144,1024]{1,0:T(8,128)(2,1)S(1)}, bf16[144,1024]{1,0:T(8,128)(2,1)S(1)}, u32[]{:S(2)}, u32[]{:S(2)}) collective-permute-start(bf16[144,1024]{1,0:T(8,128)(2,1)S(1)} %pad_maximum_fusion.1), channel_id=1, source_target_pairs={{8,0},{16,8},{24,16},{32,24},{40,32},{48,40},{56,48},{72,64},{80,7... | collective-permute-start | bytes 884744 | tf_op jit(solution)/shard_map/ppermute | solution.py:267
  4.5 1.3 collective-permute-start.7
  5.8 5.4 %collective-permute-start = (bf16[144,1024]{1,0:T(8,128)(2,1)S(1)}, bf16[144,1024]{1,0:T(8,128)(2,1)S(1)}, u32[]{:S(2)}, u32[]{:S(2)}) collective-permute-start(bf16[144,1024]{1,0:T(8,128)(2,1)S(1)} %pad_maximum_fusion.1), channel_id=1, source_target_pairs={{8,40},{72,104},{136,168},{200,232},{264,296},{328,360},{392,424},... | collective-permute-start | bytes 884744 | tf_op jit(solution)/shard_map/ppermute | solution.py:267
  16.0 1.4 collective-permute-start.1
  18.8 2.5 %constant_dynamic-slice_fusion = (bf16[2,512,128]{2,1,0:T(8,128)(2,1)S(1)}, bf16[2,512,128]{2,1,0:T(8,128)(2,1)S(1)}, bf16[2,512,128]{2,1,0:T(8,128)(2,1)S(1)}, ...) fusion(bf16[2,512,1024]{2,1,0:T(8,128)(2,1)} %param.6, ...), kind=kLoop, calls=%fused_computation.22 | loop fusion | bytes 4194336 | tf_op jit(solution)/shard_map/dynamic_slice | solution.py:290
  23.3 6.1 %collective-permute-start.14 = (bf16[2,512,128]{2,1,0:T(8,128)(2,1)S(1)}, bf16[2,512,128]{2,1,0:T(8,128)(2,1)}, u32[]{:S(2)}, u32[]{:S(2)}) collective-permute-start(bf16[2,512,128]{2,1,0:T(8,128)(2,1)S(1)} %get-tuple-element.57), channel_id=1, source_target_pairs={{0,6},{1,7},{2,4},{3,5},{4,2},{5,3},{6,0},{7,1},{8,14},{9,15},{10,... | collective-permute-start | bytes 786440 | tf_op jit(solution)/shard_map/ppermute | solution.py:294
  30.1 3.3 %collective-permute-start.12 = (bf16[2,512,128]{2,1,0:T(8,128)(2,1)S(1)}, bf16[2,512,128]{2,1,0:T(8,128)(2,1)}, u32[]{:S(2)}, u32[]{:S(2)}) collective-permute-start(bf16[2,512,128]{2,1,0:T(8,128)(2,1)S(1)} %get-tuple-element.58), channel_id=1, source_target_pairs={{0,5},{1,4},{2,7},{3,6},{4,1},{5,0},{6,3},{7,2},{8,13},{9,12},{10,... | collective-permute-start | bytes 786440 | tf_op jit(solution)/shard_map/ppermute | solution.py:294
  33.4 5.3 %collective-permute-start.10 = (bf16[2,512,128]{2,1,0:T(8,128)(2,1)}, bf16[2,512,128]{2,1,0:T(8,128)(2,1)}, u32[]{:S(2)}, u32[]{:S(2)}) collective-permute-start(bf16[2,512,128]{2,1,0:T(8,128)(2,1)} %get-tuple-element.60), channel_id=1, source_target_pairs={{0,2},{1,3},{2,0},{3,1},{4,6},{5,7},{6,4},{7,5},{8,10},{9,11},{10,... | collective-permute-start | bytes 786440 | tf_op jit(solution)/shard_map/ppermute | solution.py:294
  38.8 6.8 %collective-permute-start.9 = (bf16[2,512,128]{2,1,0:T(8,128)(2,1)}, bf16[2,512,128]{2,1,0:T(8,128)(2,1)S(1)}, u32[]{:S(2)}, u32[]{:S(2)}) collective-permute-start(bf16[2,512,128]{2,1,0:T(8,128)(2,1)} %get-tuple-element.61), channel_id=1, source_target_pairs={{0,4},{1,5},{2,6},{3,7},{4,0},{5,1},{6,2},{7,3},{8,12},{9,13},{10,... | collective-permute-start | bytes 786440 | tf_op jit(solution)/shard_map/ppermute | solution.py:294
  45.7 2.6 %collective-permute-start.8 = (bf16[2,512,128]{2,1,0:T(8,128)(2,1)S(1)}, bf16[2,512,128]{2,1,0:T(8,128)(2,1)}, u32[]{:S(2)}, u32[]{:S(2)}) collective-permute-start(bf16[2,512,128]{2,1,0:T(8,128)(2,1)S(1)} %get-tuple-element.62), channel_id=1, source_target_pairs={{0,1},{1,0},{2,3},{3,2},{4,5},{5,4},{6,7},{7,6},{8,9},{9,8},{10,11... | collective-permute-start | bytes 786440 | tf_op jit(solution)/shard_map/ppermute | solution.py:294
  49.5 10.4 %collective-permute-done.10.refs_3_ = bf16[2,512,128]{2,1,0:T(8,128)(2,1)} collective-permute-done((bf16[2,512,128]{2,1,0:T(8,128)(2,1)}, bf16[2,512,128]{2,1,0:T(8,128)(2,1)}, u32[]{:S(2)}, u32[]{:S(2)}) %collective-permute-start.10) | collective-permute-done | bytes 262176 | tf_op jit(solution)/shard_map/ppermute | solution.py:294
  59.8 1.9 collective-permute-start.11
  61.8 55.5 %collective-permute-done.9.refs_2_ = bf16[2,512,128]{2,1,0:T(8,128)(2,1)S(1)} collective-permute-done((bf16[2,512,128]{2,1,0:T(8,128)(2,1)}, bf16[2,512,128]{2,1,0:T(8,128)(2,1)S(1)}, u32[]{:S(2)}, u32[]{:S(2)}) %collective-permute-start.9) | collective-permute-done | bytes 262176 | tf_op jit(solution)/shard_map/ppermute | solution.py:294
  117.2 1.9 collective-permute-start.13
  119.2 14.4 %flash_part.2 = (f32[8,512,256]{2,1,0:T(8,128)}, f32[8,512,128]{2,1,0:T(8,128)}) custom-call(s32[8]{0:T(128)} %compare_convert_fusion.wanted_ref, f32[1,2048]{1,0:T(1,128)} %bitcast.38, bf16[4,144,1024]{2,1,0:T(8,128)(2,1)} %copy-done, bf16[2,512,128]{2,1,0:T(8,128)(2,1)} %get-tuple-element.63.refs_0_, bf16[2,512,128]{2,1,0:T(8,128)(2,1)} %collective-permute-done.8.refs_1_, ...), custom_call_target="tpu_custom_call" | custom-call | flops 8589934592 | bytes 1048576 | tf_op jit(solution)/shard_map/flash_part/pallas_call | solution.py:134
  133.8 2.4 %own_part.1 = (f32[2,64,1024]{2,1,0:T(8,128)}, f32[2,64,128]{2,1,0:T(8,128)}) custom-call(bf16[2,64,1024]{2,1,0:T(8,128)(2,1)} %q_ref, bf16[2,2,64,128]{3,2,1,0:T(8,128)(2,1)} %new_ref), custom_call_target="tpu_custom_call" | custom-call | tf_op jit(solution)/shard_map/own_part/pallas_call | solution.py:182
  136.9 14.1 %flash_part.3 = (f32[8,512,256]{2,1,0:T(8,128)}, f32[8,512,128]{2,1,0:T(8,128)}) custom-call(s32[8]{0:T(128)} %compare_convert_fusion.wanted_ref, f32[1,1536]{1,0:T(1,128)} %broadcast_in_dim.82.bias_ref, bf16[4,144,1024]{2,1,0:T(8,128)(2,1)} %copy-done, bf16[2,512,128]{2,1,0:T(8,128)(2,1)} %collective-permute-done.12.refs_0_, ...), custom_call_target="tpu_custom_call" | custom-call | flops 6442450944 | bytes 786432 | tf_op jit(solution)/shard_map/flash_part/pallas_call | solution.py:134
  151.7 7.5 %flash_last.3 = (bf16[128,1152]{1,0:T(8,128)(2,1)}, bf16[128,1152]{1,0:T(8,128)(2,1)}, bf16[128,1152]{1,0:T(8,128)(2,1)}) custom-call(s32[8]{0:T(128)} %compare_convert_fusion.wanted_ref, f32[1,512]{1,0:T(1,128)} %bitcast.36, bf16[4,144,1024]{2,1,0:T(8,128)(2,1)} %copy-done, bf16[2,512,128]{2,1,0:T(8,128)(2,1)} %copy-done.1, ...), custom_call_target="tpu_custom_call" | custom-call | flops 1610612736 | bytes 262144 | tf_op jit(solution)/shard_map/flash_last/pallas_call | solution.py:134
  160.6 3.0 %collective-permute-start.15 = (bf16[128,1152]{1,0:T(8,128)(2,1)}, bf16[128,1152]{1,0:T(8,128)(2,1)S(1)}, u32[]{:S(2)}, u32[]{:S(2)}) collective-permute-start(bf16[128,1152]{1,0:T(8,128)(2,1)} %get-tuple-element.51), channel_id=1, source_target_pairs={{0,8},{8,16},{16,24},{24,32},{32,40},{40,48},{48,56},{64,72},{72,8... | collective-permute-start | bytes 884744 | tf_op jit(solution)/shard_map/ppermute | solution.py:267
  163.6 2.2 collective-permute-start.16
  166.5 22.0 %collective-permute-start.17 = (bf16[128,1152]{1,0:T(8,128)(2,1)}, bf16[128,1152]{1,0:T(8,128)(2,1)S(1)}, u32[]{:S(2)}, u32[]{:S(2)}) collective-permute-start(bf16[128,1152]{1,0:T(8,128)(2,1)} %get-tuple-element.53), channel_id=1, source_target_pairs={{0,24},{8,32},{16,40},{24,48},{32,56},{64,88},{72,96},{80,104},{88... | collective-permute-start | bytes 884744 | tf_op jit(solution)/shard_map/ppermute | solution.py:267
  191.0 4.8 %flash_last.2.m0 = bf16[128,1152]{1,0:T(8,128)(2,1)} custom-call(s32[8]{0:T(128)} %compare_convert_fusion.wanted_ref, f32[1,512]{1,0:T(1,128)} %bitcast.37, bf16[4,144,1024]{2,1,0:T(8,128)(2,1)} %copy-done, bf16[2,512,128]{2,1,0:T(8,128)(2,1)} %copy-done.1, f32[8,512,256]{2,1,0:T(8,128)} %get-tuple-element.49.refs_1_, f32[8,512,128]{2,1,0:T(8,128)} %get-tuple-element.50.refs_2_), custom_call_target="tpu_custom_call" | custom-call | flops 536870912 | bytes 262144 | tf_op jit(solution)/shard_map/flash_last/pallas_call | solution.py:134
  195.9 24.0 %collective-permute-done.20.m4 = bf16[128,1152]{1,0:T(8,128)(2,1)S(1)} collective-permute-done((bf16[128,1152]{1,0:T(8,128)(2,1)S(1)}, bf16[128,1152]{1,0:T(8,128)(2,1)S(1)}, u32[]{:S(2)}, u32[]{:S(2)}) %collective-permute-start.20) | collective-permute-done | bytes 294944 | tf_op jit(solution)/shard_map/ppermute | solution.py:273
  220.7 3.3 %merge.1 = bf16[2,64,1024]{2,1,0:T(8,128)(2,1)} custom-call(s32[2]{0:T(128)} %compare_select_fusion.code_ref, bf16[128,1152]{1,0:T(8,128)(2,1)} %flash_last.2.m0, bf16[128,1152]{1,0:T(8,128)(2,1)} %copy-done.2, bf16[128,1152]{1,0:T(8,128)(2,1)} %copy-done.3, bf16[128,1152]{1,0:T(8,128)(2,1)} %copy-done.5, bf16[128,1152]{1,0:T(8,128)(2,1)} %copy-done.6, ...), custom_call_target="tpu_custom_call" | custom-call | tf_op jit(solution)/shard_map/merge/pallas_call | solution.py:227
  (78 shorter events, 17.9 us)
Async XLA Ops:
  1.9 28.2 %collective-permute-start.3 = (bf16[144,1024]{1,0:T(8,128)(2,1)S(1)}, bf16[144,1024]{1,0:T(8,128)(2,1)S(1)}, u32[]{:S(2)}, u32[]{:S(2)}) collective-permute-start(bf16[144,1024]{1,0:T(8,128)(2,1)S(1)} %pad_maximum_fusion.1), channel_id=1, source_target_pairs={{8,0},{16,8},{24,16},{32,24},{40,32},{48,40},{56,48},{72,64},{80,7... | collective-permute-start | bytes 884744 | tf_op jit(solution)/shard_map/ppermute | solution.py:267
  4.5 18.8 %collective-permute-start.7 = (bf16[144,1024]{1,0:T(8,128)(2,1)S(1)}, bf16[144,1024]{1,0:T(8,128)(2,1)S(1)}, u32[]{:S(2)}, u32[]{:S(2)}) collective-permute-start(bf16[144,1024]{1,0:T(8,128)(2,1)S(1)} %pad_maximum_fusion.1), channel_id=1, source_target_pairs={{24,0},{32,8},{40,16},{48,24},{56,32},{88,64},{96,72},{104,80},{11... | collective-permute-start | bytes 884744 | tf_op jit(solution)/shard_map/ppermute | solution.py:267
  5.8 9.1 %collective-permute-start = (bf16[144,1024]{1,0:T(8,128)(2,1)S(1)}, bf16[144,1024]{1,0:T(8,128)(2,1)S(1)}, u32[]{:S(2)}, u32[]{:S(2)}) collective-permute-start(bf16[144,1024]{1,0:T(8,128)(2,1)S(1)} %pad_maximum_fusion.1), channel_id=1, source_target_pairs={{8,40},{72,104},{136,168},{200,232},{264,296},{328,360},{392,424},... | collective-permute-start | bytes 884744 | tf_op jit(solution)/shard_map/ppermute | solution.py:267
  11.2 27.6 %collective-permute-start.5 = (bf16[144,1024]{1,0:T(8,128)(2,1)S(1)}, bf16[144,1024]{1,0:T(8,128)(2,1)S(1)}, u32[]{:S(2)}, u32[]{:S(2)}) collective-permute-start(bf16[144,1024]{1,0:T(8,128)(2,1)S(1)} %pad_maximum_fusion.1), channel_id=1, source_target_pairs={{16,0},{24,8},{32,16},{40,24},{48,32},{56,40},{80,64},{88,72},{96,... | collective-permute-start | bytes 884744 | tf_op jit(solution)/shard_map/ppermute | solution.py:267
  16.0 2.0 collective-permute-start.1
  18.0 11.3 %collective-permute-start.6 = (bf16[144,1024]{1,0:T(8,128)(2,1)}, bf16[144,1024]{1,0:T(8,128)(2,1)S(1)}, u32[]{:S(2)}, u32[]{:S(2)}) collective-permute-start(bf16[144,1024]{1,0:T(8,128)(2,1)} %collective-permute-done.1), channel_id=1, source_target_pairs={{0,40},{40,48},{16,56},{64,104},{104,112},{80,120},{128,168},{168,... | collective-permute-start | bytes 884744 | tf_op jit(solution)/shard_map/ppermute | solution.py:267
  21.3 12.1 %collective-permute-start.2 = (bf16[144,1024]{1,0:T(8,128)(2,1)}, bf16[144,1024]{1,0:T(8,128)(2,1)S(1)}, u32[]{:S(2)}, u32[]{:S(2)}) collective-permute-start(bf16[144,1024]{1,0:T(8,128)(2,1)} %collective-permute-done.1), channel_id=1, source_target_pairs={{0,56},{64,120},{128,184},{192,248},{256,312},{320,376},{384,440},... | collective-permute-start | bytes 884744 | tf_op jit(solution)/shard_map/ppermute | solution.py:267
  23.3 113.6 %collective-permute-start.14 = (bf16[2,512,128]{2,1,0:T(8,128)(2,1)S(1)}, bf16[2,512,128]{2,1,0:T(8,128)(2,1)}, u32[]{:S(2)}, u32[]{:S(2)}) collective-permute-start(bf16[2,512,128]{2,1,0:T(8,128)(2,1)S(1)} %get-tuple-element.57), channel_id=1, source_target_pairs={{0,6},{1,7},{2,4},{3,5},{4,2},{5,3},{6,0},{7,1},{8,14},{9,15},{10,... | collective-permute-start | bytes 786440 | tf_op jit(solution)/shard_map/ppermute | solution.py:294
  29.4 16.3 %collective-permute-start.4 = (bf16[144,1024]{1,0:T(8,128)(2,1)}, bf16[144,1024]{1,0:T(8,128)(2,1)S(1)}, u32[]{:S(2)}, u32[]{:S(2)}) collective-permute-start(bf16[144,1024]{1,0:T(8,128)(2,1)} %collective-permute-done.1), channel_id=1, source_target_pairs={{0,48},{40,56},{64,112},{104,120},{128,176},{168,184},{192,240},{2... | collective-permute-start | bytes 884744 | tf_op jit(solution)/shard_map/ppermute | solution.py:267
  30.1 106.7 %collective-permute-start.12 = (bf16[2,512,128]{2,1,0:T(8,128)(2,1)S(1)}, bf16[2,512,128]{2,1,0:T(8,128)(2,1)}, u32[]{:S(2)}, u32[]{:S(2)}) collective-permute-start(bf16[2,512,128]{2,1,0:T(8,128)(2,1)S(1)} %get-tuple-element.58), channel_id=1, source_target_pairs={{0,5},{1,4},{2,7},{3,6},{4,1},{5,0},{6,3},{7,2},{8,13},{9,12},{10,... | collective-permute-start | bytes 786440 | tf_op jit(solution)/shard_map/ppermute | solution.py:294
  33.4 26.4 %collective-permute-start.10 = (bf16[2,512,128]{2,1,0:T(8,128)(2,1)}, bf16[2,512,128]{2,1,0:T(8,128)(2,1)}, u32[]{:S(2)}, u32[]{:S(2)}) collective-permute-start(bf16[2,512,128]{2,1,0:T(8,128)(2,1)} %get-tuple-element.60), channel_id=1, source_target_pairs={{0,2},{1,3},{2,0},{3,1},{4,6},{5,7},{6,4},{7,5},{8,10},{9,11},{10,... | collective-permute-start | bytes 786440 | tf_op jit(solution)/shard_map/ppermute | solution.py:294
  38.8 78.4 %collective-permute-start.9 = (bf16[2,512,128]{2,1,0:T(8,128)(2,1)}, bf16[2,512,128]{2,1,0:T(8,128)(2,1)S(1)}, u32[]{:S(2)}, u32[]{:S(2)}) collective-permute-start(bf16[2,512,128]{2,1,0:T(8,128)(2,1)} %get-tuple-element.61), channel_id=1, source_target_pairs={{0,4},{1,5},{2,6},{3,7},{4,0},{5,1},{6,2},{7,3},{8,12},{9,13},{10,... | collective-permute-start | bytes 786440 | tf_op jit(solution)/shard_map/ppermute | solution.py:294
  45.7 73.5 %collective-permute-start.8 = (bf16[2,512,128]{2,1,0:T(8,128)(2,1)S(1)}, bf16[2,512,128]{2,1,0:T(8,128)(2,1)}, u32[]{:S(2)}, u32[]{:S(2)}) collective-permute-start(bf16[2,512,128]{2,1,0:T(8,128)(2,1)S(1)} %get-tuple-element.62), channel_id=1, source_target_pairs={{0,1},{1,0},{2,3},{3,2},{4,5},{5,4},{6,7},{7,6},{8,9},{9,8},{10,11... | collective-permute-start | bytes 786440 | tf_op jit(solution)/shard_map/ppermute | solution.py:294
  48.5 70.7 %copy-start = (bf16[4,144,1024]{2,1,0:T(8,128)(2,1)}, bf16[4,144,1024]{2,1,0:T(8,128)(2,1)S(1)}, u32[]{:S(2)}) copy-start(bf16[4,144,1024]{2,1,0:T(8,128)(2,1)S(1)} %pad_maximum_fusion.q_ref) | copy-start | bytes 3538948
  59.8 91.1 %collective-permute-start.11 = (bf16[2,512,128]{2,1,0:T(8,128)(2,1)S(1)}, bf16[2,512,128]{2,1,0:T(8,128)(2,1)S(1)}, u32[]{:S(2)}, u32[]{:S(2)}) collective-permute-start(bf16[2,512,128]{2,1,0:T(8,128)(2,1)S(1)} %get-tuple-element.59), channel_id=1, source_target_pairs={{0,7},{1,6},{2,5},{3,4},{4,3},{5,2},{6,1},{7,0},{8,15},{9,14},{10,... | collective-permute-start | bytes 786440 | tf_op jit(solution)/shard_map/ppermute | solution.py:294
  117.2 19.6 %collective-permute-start.13 = (bf16[2,512,128]{2,1,0:T(8,128)(2,1)S(1)}, bf16[2,512,128]{2,1,0:T(8,128)(2,1)}, u32[]{:S(2)}, u32[]{:S(2)}) collective-permute-start(bf16[2,512,128]{2,1,0:T(8,128)(2,1)S(1)} %get-tuple-element.64), channel_id=1, source_target_pairs={{0,3},{1,2},{2,1},{3,0},{4,7},{5,6},{6,5},{7,4},{8,11},{9,10},{10,... | collective-permute-start | bytes 786440 | tf_op jit(solution)/shard_map/ppermute | solution.py:294
  159.2 7.3 %collective-permute-start.18 = (bf16[128,1152]{1,0:T(8,128)(2,1)}, bf16[128,1152]{1,0:T(8,128)(2,1)S(1)}, u32[]{:S(2)}, u32[]{:S(2)}) collective-permute-start(bf16[128,1152]{1,0:T(8,128)(2,1)} %get-tuple-element.51), channel_id=1, source_target_pairs={{56,40},{120,104},{184,168},{248,232},{312,296},{376,360},{440,424... | collective-permute-start | bytes 884744 | tf_op jit(solution)/shard_map/ppermute | solution.py:267
  159.9 28.7 %collective-permute-start.19 = (bf16[128,1152]{1,0:T(8,128)(2,1)}, bf16[128,1152]{1,0:T(8,128)(2,1)S(1)}, u32[]{:S(2)}, u32[]{:S(2)}) collective-permute-start(bf16[128,1152]{1,0:T(8,128)(2,1)} %get-tuple-element.52), channel_id=1, source_target_pairs={{48,40},{56,48},{112,104},{120,112},{176,168},{184,176},{240,232},... | collective-permute-start | bytes 884744 | tf_op jit(solution)/shard_map/ppermute | solution.py:267
  160.6 35.3 %collective-permute-start.15 = (bf16[128,1152]{1,0:T(8,128)(2,1)}, bf16[128,1152]{1,0:T(8,128)(2,1)S(1)}, u32[]{:S(2)}, u32[]{:S(2)}) collective-permute-start(bf16[128,1152]{1,0:T(8,128)(2,1)} %get-tuple-element.51), channel_id=1, source_target_pairs={{0,8},{8,16},{16,24},{24,32},{32,40},{40,48},{48,56},{64,72},{72,8... | collective-permute-start | bytes 884744 | tf_op jit(solution)/shard_map/ppermute | solution.py:267
  163.6 32.3 %collective-permute-start.16 = (bf16[128,1152]{1,0:T(8,128)(2,1)}, bf16[128,1152]{1,0:T(8,128)(2,1)S(1)}, u32[]{:S(2)}, u32[]{:S(2)}) collective-permute-start(bf16[128,1152]{1,0:T(8,128)(2,1)} %get-tuple-element.52), channel_id=1, source_target_pairs={{0,16},{8,24},{16,32},{24,40},{32,48},{40,56},{64,80},{72,88},{80,... | collective-permute-start | bytes 884744 | tf_op jit(solution)/shard_map/ppermute | solution.py:267
  165.8 30.0 %collective-permute-start.21 = (bf16[128,1152]{1,0:T(8,128)(2,1)}, bf16[128,1152]{1,0:T(8,128)(2,1)S(1)}, u32[]{:S(2)}, u32[]{:S(2)}) collective-permute-start(bf16[128,1152]{1,0:T(8,128)(2,1)} %get-tuple-element.53), channel_id=1, source_target_pairs={{56,80},{120,144},{184,208},{248,272},{312,336},{376,400},{440,464... | collective-permute-start | bytes 884744 | tf_op jit(solution)/shard_map/ppermute | solution.py:273
  166.5 29.4 %collective-permute-start.17 = (bf16[128,1152]{1,0:T(8,128)(2,1)}, bf16[128,1152]{1,0:T(8,128)(2,1)S(1)}, u32[]{:S(2)}, u32[]{:S(2)}) collective-permute-start(bf16[128,1152]{1,0:T(8,128)(2,1)} %get-tuple-element.53), channel_id=1, source_target_pairs={{0,24},{8,32},{16,40},{24,48},{32,56},{64,88},{72,96},{80,104},{88... | collective-permute-start | bytes 884744 | tf_op jit(solution)/shard_map/ppermute | solution.py:267
  189.7 30.2 %collective-permute-start.20 = (bf16[128,1152]{1,0:T(8,128)(2,1)S(1)}, bf16[128,1152]{1,0:T(8,128)(2,1)S(1)}, u32[]{:S(2)}, u32[]{:S(2)}) collective-permute-start(bf16[128,1152]{1,0:T(8,128)(2,1)S(1)} %select_select_fusion), channel_id=1, source_target_pairs={{40,64},{48,72},{104,128},{112,136},{168,192},{176,200},{232,256},... | collective-permute-start | bytes 884744 | tf_op jit(solution)/shard_map/ppermute | solution.py:273
  195.8 24.1 %copy-start.2 = (bf16[128,1152]{1,0:T(8,128)(2,1)}, bf16[128,1152]{1,0:T(8,128)(2,1)S(1)}, u32[]{:S(2)}) copy-start(bf16[128,1152]{1,0:T(8,128)(2,1)S(1)} %collective-permute-done.15.m1) | copy-start | bytes 884740
  (7 other events, 92.6 us)
